TPU v7x, 512 devices: a whole 4x4x16 slice. The times are simulated.
512 devices in a mesh: dp: 64 (over y_lo, z, core), mp: 8 (over y_hi, x).
Axes of the slice: x: 4, y: 4 (y_hi: 2, y_lo: 2; y = y_hi * 2 + y_lo), z: 16, core: 2. Of those that a mesh axis runs over, the one named last changes fastest.
Arguments:
- hidden_in: bfloat16 [32768, 4096], P('dp'), may hold values from -1.5 to 1.5
- w_query: bfloat16 [4096, 4096], P('dp', 'mp'), may hold values from -1 to 1
- w_key: bfloat16 [4096, 1024], P('dp', 'mp'), may hold values from -24 to 24
- w_value: bfloat16 [4096, 1024], P('dp', 'mp'), may hold values from -1 to 1
- w_out: bfloat16 [4096, 4096], P('dp', 'mp'), may hold values from -1 to 1
- value_weight: float32 [4096], P('mp'), may hold values from -0.09375 to 0.09375
- rewards: float32 [32768], P('dp'), may hold values from -0.6 to 0.6
- old_values: float32 [32768], P('dp'), may hold values from -6 to 6
- lengths: int32 [256], replicated, may hold values from 1 to 2048, 32768 in all
- terminal: int32 [256], replicated, may hold values 0 or 1
Outputs:
- value: float32 [32768], P('dp')
- advantage: float32 [32768], P('dp')
- value_loss: float32 [], replicated
All inputs are finite; a program needn't handle non-finite values.
Results may differ from a plain program's by a relative error of at most 0.012.
The roundings to bfloat16 on the way count: a program that leaves them out, or rounds other values in their place, can miss the bound.
Values may be sent and summed in bfloat16 or wider, within the bound.
A program may use at most 128 MiB of HBM per device.

v0:
```python
import jax
import jax.numpy as jnp
from jax import lax
from jax.sharding import PartitionSpec as P

HEAD = 128


discount = 0.999
trace_decay = 0.997
clip_range = 0.2
epsilon = 1e-05
rope_base = 500000.0


def sent_together(arrays, axis, dim, along):
    widths = [a.shape[along] for a in arrays]
    both = jnp.concatenate(arrays, axis=along)
    whole = lax.all_gather(both, axis, axis=dim, tiled=True)
    return tuple(jnp.split(whole, [sum(widths[:k]) for k in range(1, len(widths))], axis=along))


def from_everyone(array, axis):
    size = lax.axis_size(axis)
    return lax.all_to_all(
        jnp.broadcast_to(array[None], (size, *array.shape)), axis, 0, 0, tiled=True
    )


def of_everyone(array, axis):
    everything = from_everyone(array, axis)
    return jnp.sum(everything, axis=0)


def in_one(arrays, axis):
    ends = [0]
    for a in arrays:
        ends.append(ends[-1] + a.size)
    total = of_everyone(jnp.concatenate([a.ravel() for a in arrays]), axis)
    return tuple((total[b:e].reshape(a.shape) for a, b, e in zip(arrays, ends, ends[1:])))


def from_behind(array, axis, by):
    size = lax.axis_size(axis)
    pairs = [(i, i + by) for i in range(size) if 0 <= i + by < size]
    return lax.ppermute(array, axis, pairs)


def collected_together(array, axis):
    leaves = jax.tree.leaves(array)
    order = sorted(range(len(leaves)), key=lambda k: -leaves[k].size)
    width = (1, *leaves[order[0]].shape)[-1]
    lines = [
        jnp.pad(leaves[k].reshape(-1), (0, -leaves[k].size % width)).reshape(-1, width)
        for k in order
    ]
    both, at, found = (from_everyone(jnp.concatenate(lines), axis), 0, {})
    for k, line in zip(order, lines):
        slab = both[:, at : at + len(line)].reshape(len(both), -1)
        found[k] = slab[:, : leaves[k].size].reshape(-1, *leaves[k].shape)
        at += len(line)
    numbers = iter(range(len(leaves)))
    return jax.tree.map(lambda _: found[next(numbers)], array)


def joined_by_halves(pieces, combine):
    while len(jax.tree.leaves(pieces)[0]) > 1:
        pieces = jax.vmap(combine)(
            *(jax.tree.map(lambda part: part[side::2], pieces) for side in (0, 1))
        )
    return jax.tree.map(lambda part: part[0], pieces)


def prefix_2(array, axis, combine, identity):
    size, mine = (lax.axis_size(axis), lax.axis_index(axis))
    passed = jnp.arange(size) > mine

    def kept(part, zero, own):
        part = jnp.where(
            passed.reshape(-1, *(1 for _ in own.shape)), part, jnp.asarray(zero, own.dtype)
        )
        return part[::-1]

    pieces = collected_together(array, axis)
    return joined_by_halves(jax.tree.map(kept, pieces, identity, array), combine)


def rotate(states, positions):
    half = HEAD // 2
    freq = rope_base ** (-jnp.arange(half, dtype=jnp.float32) * 2.0 / HEAD)
    angles = positions[:, None] * freq[None, :]
    cosine = jnp.cos(angles)[:, None, :]
    sine = jnp.sin(angles)[:, None, :]
    first = states[..., :half]
    second = states[..., half:]
    return jnp.concatenate([first * cosine - second * sine, second * cosine + first * sine], -1)


def body(
    hidden_in, w_query, w_key, w_value, w_out, value_weight, rewards, old_values, lengths, terminal
):
    rows = hidden_in.shape[0]
    width = hidden_in.shape[1]
    states = hidden_in.astype(jnp.float32)
    normed = (states * lax.rsqrt(jnp.mean(states * states, 1, keepdims=True) + epsilon)).astype(
        jnp.bfloat16
    )
    pieces = sent_together((w_query, w_key, w_value, w_out), "dp", 0, 1)
    add_pieces = pieces[:3]
    summed = tuple(
        (jnp.dot(normed, piece, preferred_element_type=jnp.float32) for piece in add_pieces)
    )
    stored = pieces[3]
    query_sum, key_sum, value_sum, whole_out = summed + (stored,)
    position_ids = lax.axis_index("dp") * rows + jnp.arange(rows, dtype=jnp.int32)
    positions = position_ids.astype(jnp.float32)
    local_heads = w_query.shape[1] // HEAD
    local_kv = w_key.shape[1] // HEAD
    group = local_heads // local_kv
    query = rotate(query_sum.reshape(rows, local_heads, HEAD), positions).astype(jnp.bfloat16)
    key = rotate(key_sum.reshape(rows, local_kv, HEAD), positions).astype(jnp.bfloat16)
    values_proj = value_sum.astype(jnp.bfloat16).reshape(rows, local_kv, HEAD)
    ends = jnp.cumsum(lengths)
    matches = ends[None, :] - 1 == position_ids[:, None]
    finished = jnp.any(matches, 1).astype(jnp.float32)
    stopped = jnp.sum(jnp.where(matches, terminal[None, :], 0), 1).astype(jnp.float32)
    episode = jnp.sum((ends[None, :] <= position_ids[:, None]).astype(jnp.int32), 1)
    order = jnp.arange(rows, dtype=jnp.int32)
    same_episode = episode[None, :] == episode[:, None]
    allowed = (order[None, :] <= order[:, None]) & same_episode
    scores = jnp.einsum(
        "tkgd,skd->kgts",
        query.reshape(rows, local_kv, group, HEAD),
        key,
        preferred_element_type=jnp.float32,
    ) * (1.0 / HEAD**0.5)
    masked = jnp.where(allowed[None, None], scores, -1e30)
    largest = jnp.max(masked, -1, keepdims=True)
    expon = jnp.where(allowed[None, None], jnp.exp(masked - largest), 0.0)
    probs = (expon / jnp.sum(expon, -1, keepdims=True)).astype(jnp.bfloat16)
    output = jnp.einsum("kgts,skd->tkgd", probs, values_proj, preferred_element_type=jnp.float32)
    attended = output.astype(jnp.bfloat16).reshape(rows, local_heads * HEAD)
    all_heads = lax.all_gather(attended, "mp", axis=1, tiled=True)
    projected = jnp.dot(all_heads, whole_out, preferred_element_type=jnp.float32)
    feature_count = w_out.shape[1]
    own_states = lax.dynamic_slice_in_dim(
        states, lax.axis_index("mp") * feature_count, feature_count, 1
    )
    residual = own_states + projected
    square_sum, head_sum = in_one(
        (jnp.sum(residual * residual, 1), jnp.sum(residual * value_weight[None, :], 1)), "mp"
    )
    value = head_sum * lax.rsqrt(square_sum / width + epsilon)
    following = from_behind(old_values[:1], "dp", -1)
    next_old = jnp.concatenate([old_values[1:], following])
    booted = jnp.where(finished > 0, (1.0 - stopped) * old_values, next_old)
    delta = rewards + discount * booted - old_values
    keep_rate = discount * trace_decay
    spacing = (order[None, :] - order[:, None]).astype(jnp.float32)
    forward_mask = (spacing >= 0.0) & same_episode
    decay_matrix = jnp.where(
        forward_mask, jnp.power(jnp.float32(keep_rate), jnp.maximum(spacing, 0.0)), 0.0
    )
    local_part = jnp.dot(decay_matrix, delta, precision=lax.Precision.HIGHEST)
    remaining = (rows - order).astype(jnp.float32)
    reach = jnp.where(episode == episode[-1], jnp.power(jnp.float32(keep_rate), remaining), 0.0) * (
        1.0 - finished[-1]
    )

    def compose(earlier, later_map):
        return (later_map[0] + later_map[1] * earlier[0], later_map[1] * earlier[1])

    prefix = prefix_2(
        (local_part[:1], reach[:1]),
        "dp",
        compose,
        (jnp.zeros((1,), jnp.float32), jnp.ones((1,), jnp.float32)),
    )
    incoming = prefix[0][0]
    advantage = local_part + reach * incoming
    returns = advantage + old_values
    clipped = old_values + jnp.clip(value - old_values, -clip_range, clip_range)
    terms = jnp.maximum((value - returns) ** 2, (clipped - returns) ** 2)
    total_loss = of_everyone(jnp.sum(terms), "dp")
    value_loss = 0.5 * total_loss / (rows * lax.axis_size("dp"))
    return (value, advantage, value_loss)


def solution(mesh):
    return jax.shard_map(
        body,
        mesh=mesh,
        in_specs=(
            P("dp", None),
            P("dp", "mp"),
            P("dp", "mp"),
            P("dp", "mp"),
            P("dp", "mp"),
            P("mp"),
            P("dp"),
            P("dp"),
            P(),
            P(),
        ),
        out_specs=(P("dp"), P("dp"), P()),
        check_vma=False,
    )
```

profile of v0, /device:TPU:1, one launch (start us, length us, event | category | flops | bytes accessed | tf_op | source)
XLA Modules:
  0.0 308.6 jit_solution(11443152681858207137)
XLA Ops:
  7.2 1.6 pad_maximum_fusion
  8.9 1.0 reduce-window.9
  10.0 6.5 %copy.47 = bf16[512,4096]{0,1:T(8,128)(2,1)} copy(bf16[512,4096]{1,0:T(8,128)(2,1)} %param.10) | data formatting | bytes 8388608 | tf_op args[0]
  16.7 0.3 fusion.29
  17.0 3.1 %multiply_reduce_fusion = f32[512]{0:T(512)S(1)} fusion(bf16[512,4096]{0,1:T(8,128)(2,1)} %copy.47), kind=kLoop, calls=%fused_computation.1 | loop fusion | flops 6290944 | bytes 4196352 | tf_op jit(solution)/shard_map/reduce_sum | solution.py:105
  20.2 0.2 compare_and_fusion.1
  20.4 1.0 multiply_cosine_fusion
  21.4 125.4 %all-gather.3.cloned.1.call-done = bf16[4096,1280]{1,0:T(8,128)(2,1)} async-done(((bf16[64,1280]{1,0:T(8,128)(2,1)}), bf16[4096,1280]{1,0:T(8,128)(2,1)}) %all-gather.3.cloned.1.call-update) | async-done | bytes 10485776 | tf_op jit(solution)/shard_map/all_gather | solution.py:19
  146.8 3.6 %fusion.17 = f32[512,1,128]{0,2,1:T(8,128)S(1)} fusion(f32[512]{0:T(512)S(1)} %add_rsqrt_fusion, bf16[512,4096]{0,1:T(8,128)(2,1)} %copy.47, bf16[4096,1280]{1,0:T(8,128)(2,1)} %all-gather.3.cloned.1.call-done), kind=kOutput, calls=%fused_computation.20 | convolution fusion | flops 543162368 | bytes 5507072 | tf_op jit(solution)/shard_map/dot_general | solution.py:111
  150.4 0.6 fusion.49
  151.0 4.7 %fusion.2 = f32[512,512]{0,1:T(8,128)S(1)} fusion(bf16[4096,1280]{1,0:T(8,128)(2,1)} %all-gather.3.cloned.1.call-done, f32[512]{0:T(512)S(1)} %add_rsqrt_fusion, bf16[512,4096]{0,1:T(8,128)(2,1)S(1)} %copy-done), kind=kOutput, calls=%fused_computation.4 | convolution fusion | flops 2153775104 | bytes 9439232 | tf_op jit(solution)/shard_map/dot_general | solution.py:111
  155.8 0.3 copy.63
  156.1 0.3 copy.62
  156.5 0.3 subtract_convert_fusion
  156.8 1.2 fusion.4
  158.0 2.1 copy-done.1
  160.1 1.0 fusion.7
  161.1 7.6 %fusion.14 = bf16[128,4,512]{2,0,1:T(8,128)(2,1)} fusion(f32[4,512]{1,0:T(4,128)S(1)} %fusion.7, f32[4,512]{1,0:T(4,128)S(1)} %get-tuple-element.34, f32[512,512,4]{1,0,2:T(8,128)} %copy-done.1, pred[512,512]{0,1:T(8,128)(4,1)S(1)} %compare_and_fusion.1, f32[512]{0:T(512)S(1)} %copy-done.4, bf16[512,4096]{0,1:T(8,128)(2,1)} %copy.47, ...), kind=kOutput, calls=%fused_computation.19 | convolution fusion | flops 818216960 | bytes 10242048 | tf_op jit(solution)/shard_map/kgts,skd->tkgd/dot_general | solution.py:141
  168.8 0.5 slice.142
  169.3 2.2 collective-permute-start
  171.5 0.7 slice.143
  172.3 0.2 compare_reduce_fusion
  172.5 0.6 slice.144
  173.7 0.7 select_multiply_fusion
  174.4 0.5 slice.146
  175.0 0.7 fusion.52
  175.7 1.1 fusion.22
  176.8 0.5 slice.145
  177.3 1.4 maximum_bitcast_fusion.2
  178.7 0.6 broadcast_in_dim.56
  179.3 9.7 %all-to-all-start.1 = ((f32[64,2,1]{1,2,0:T(1,128)}), f32[64,2,1]{1,2,0:T(1,128)S(1)}, u32[]{:S(2)}, u32[]{:S(2)}) async-start(f32[64,2,1]{1,2,0:T(1,128)} %broadcast_in_dim.56), calls=%async_computation.1 | async-start | bytes 65536 | tf_op jit(solution)/shard_map/all_to_all | solution.py:25
  189.0 6.7 %convert_element_type.52 = f32[512,4096]{0,1:T(8,128)} convert(bf16[512,4096]{0,1:T(8,128)(2,1)} %copy.47) | non-fusion elementwise | flops 2097152 | bytes 12582912 | tf_op jit(solution)/shard_map/convert_element_type | solution.py:104
  195.8 6.6 %all-to-all-done.1 = f32[64,2,1]{1,2,0:T(1,128)S(1)} async-done(((f32[64,2,1]{1,2,0:T(1,128)}), f32[64,2,1]{1,2,0:T(1,128)S(1)}, u32[]{:S(2)}, u32[]{:S(2)}) %all-to-all-start.1) | async-done | bytes 544 | tf_op jit(solution)/shard_map/all_to_all | solution.py:25
  202.3 1.1 slice_reduce_fusion
  203.4 0.1 slice.156
  203.6 0.1 slice.151
  203.7 0.1 slice.153
  206.0 45.3 %all-gather.5.cloned.1.call-done = bf16[512,4096]{0,1:T(8,128)(2,1)} async-done(((bf16[512,512]{0,1:T(8,128)(2,1)}), bf16[512,4096]{0,1:T(8,128)(2,1)}) %all-gather.5.cloned.1.call-update) | async-done | bytes 4194320 | tf_op jit(solution)/shard_map/all_gather | solution.py:143
  251.3 6.1 %multiply_reduce_fusion.2 = (f32[512]{0:T(512)S(1)}, f32[512]{0:T(512)S(1)}) fusion(f32[512]{0:T(512)S(1)} %copy-done.7, bf16[512,4096]{0,1:T(8,128)(2,1)} %all-gather.5.cloned.1.call-done, bf16[4096,1280]{1,0:T(8,128)(2,1)} %all-gather.3.cloned.1.call-done, f32[512,4096]{0,1:T(8,128)} %convert_element_type.52, s32[]{:T(128)S(6)} %select_n.49), kind=kOutput, calls=%fused_computation.33 | convolution fusion | flops 2148793344 | bytes 9443332 | tf_op jit(solution)/shard_map/dot_general | solution.py:144
  257.4 0.6 broadcast_in_dim.51
  258.0 3.3 %all-to-all-start = ((f32[8,1,1024]{2,1,0:T(1,128)}), f32[8,1,1024]{2,1,0:T(1,128)S(1)}, u32[]{:S(2)}, u32[]{:S(2)}) async-start(f32[8,1,1024]{2,1,0:T(1,128)} %broadcast_in_dim.51), calls=%async_computation | async-start | bytes 65536 | tf_op jit(solution)/shard_map/all_to_all | solution.py:25
  261.4 0.6 fusion.61
  262.0 0.6 slice.174
  264.5 3.4 %all-to-all-done = f32[8,1,1024]{2,1,0:T(1,128)S(1)} async-done(((f32[8,1,1024]{2,1,0:T(1,128)}), f32[8,1,1024]{2,1,0:T(1,128)S(1)}, u32[]{:S(2)}, u32[]{:S(2)}) %all-to-all-start) | async-done | bytes 32800 | tf_op jit(solution)/shard_map/all_to_all | solution.py:25
  268.0 2.0 maximum_reduce_fusion
  269.9 0.7 broadcast_in_dim.96
  270.6 28.7 %all_to_all.17 = f32[64,1,1]{2,1,0:T(1,128)S(1)} all-to-all(f32[64,1,1]{2,1,0:T(1,128)S(1)} %broadcast_in_dim.96), channel_id=1, replica_groups=mesh['dp'=64,'mp'=8] {'dp'}, dimensions={0} | all-to-all | bytes 512 | tf_op jit(solution)/shard_map/all_to_all | solution.py:25
  299.3 0.7 reduce_sum.89
  (60 shorter events, 2.8 us)
Async XLA Ops:
  7.2 139.6 %all-gather.3.cloned.1.call-start = ((), (), s32[]{:S(2)}) async-start(), calls=%async_computation.3 | async-start | bytes 10649600 | tf_op jit(solution)/shard_map/all_gather | solution.py:19
  8.8 242.5 %all-gather.5.cloned.1.call-start = ((), (), s32[]{:S(2)}) async-start(), calls=%async_computation.4 | async-start | bytes 4718592 | tf_op jit(solution)/shard_map/all_gather | solution.py:143
  10.0 6.7 %copy-start.6 = (s32[256]{0:T(256)S(1)}, s32[256]{0:T(256)}, u32[]{:S(2)}) copy-start(s32[256]{0:T(256)} %param.19) | copy-start | bytes 3076
  20.1 130.8 %copy-start.3 = (f32[512]{0:T(512)}, f32[512]{0:T(512)S(1)}, u32[]{:S(2)}) copy-start(f32[512]{0:T(512)S(1)} %add_rsqrt_fusion) | copy-start | bytes 6148
  146.8 4.2 %copy-start = (bf16[512,4096]{0,1:T(8,128)(2,1)S(1)}, bf16[512,4096]{0,1:T(8,128)(2,1)}, u32[]{:S(2)}) copy-start(bf16[512,4096]{0,1:T(8,128)(2,1)} %copy.47) | copy-start | bytes 12582916
  156.8 4.4 %copy-start.4 = (f32[512]{0:T(512)S(1)}, f32[512]{0:T(512)}, u32[]{:S(2)}) copy-start(f32[512]{0:T(512)} %copy-done.3) | copy-start | bytes 6148
  158.0 2.1 copy-start.1
  161.1 7.7 %copy-start.2 = (f32[512]{0:T(512)S(1)}, f32[512]{0:T(512)}, u32[]{:S(2)}) copy-start(f32[512]{0:T(512)} %param.17) | copy-start | bytes 6148
  161.1 13.8 %copy-start.5 = (f32[512]{0:T(512)S(1)}, f32[512]{0:T(512)}, u32[]{:S(2)}) copy-start(f32[512]{0:T(512)} %param.16) | copy-start | bytes 6148
  169.3 5.6 %collective-permute-start = (f32[1]{0:T(128)}, f32[1]{0:T(128)}, u32[]{:S(2)}, u32[]{:S(2)}) collective-permute-start(f32[1]{0:T(128)} %slice.142), channel_id=1, source_target_pairs={{8,0},{16,8},{24,16},{32,24},{40,32},{48,40},{56,48},{64,56},{72,6... | collective-permute-start | bytes 20 | tf_op jit(solution)/shard_map/ppermute | solution.py:46
  179.3 23.1 %all-to-all-start.1 = ((f32[64,2,1]{1,2,0:T(1,128)}), f32[64,2,1]{1,2,0:T(1,128)S(1)}, u32[]{:S(2)}, u32[]{:S(2)}) async-start(f32[64,2,1]{1,2,0:T(1,128)} %broadcast_in_dim.56), calls=%async_computation.1 | async-start | bytes 65536 | tf_op jit(solution)/shard_map/all_to_all | solution.py:25
  189.0 62.3 %copy-start.7 = (f32[512]{0:T(512)S(1)}, f32[512]{0:T(512)}, u32[]{:S(2)}) copy-start(f32[512]{0:T(512)} %param.15) | copy-start | bytes 6148
  258.0 9.9 %all-to-all-start = ((f32[8,1,1024]{2,1,0:T(1,128)}), f32[8,1,1024]{2,1,0:T(1,128)S(1)}, u32[]{:S(2)}, u32[]{:S(2)}) async-start(f32[8,1,1024]{2,1,0:T(1,128)} %broadcast_in_dim.51), calls=%async_computation | async-start | bytes 65536 | tf_op jit(solution)/shard_map/all_to_all | solution.py:25
Sparse Core Ops, SparseCore 0:
  10.1 136.5 all-gather.2
  168.9 82.2 all-gather.4
where the time goes:
time: 309 us
  waiting for transfers between devices  181 us (59%)
  blocking collectives  28.7 us (9%)
  matrix products  24.4 us (8%)
  other arithmetic  21.7 us (7%)
  local copies, waits for them, and re-layouts  19.1 us (6%)
  between operations  18.7 us (6%)
  starting transfers between devices  15.3 us (5%)
    all_gather x1, waiting for transfers between devices, sent_together(): whole = lax.all_gather(both, axis, axis=dim, tiled=True)  125 us
    all_gather x1, waiting for transfers between devices, body(): all_heads = lax.all_gather(attended, 'mp', axis=1, tiled=True)  45.3 us
    all_to_all x1, blocking collectives, from_everyone(): lax.all_to_all(jnp.broadcast_to(array[None], (size, *array.shape)), axis,...  28.7 us
    all_to_all x2, starting transfers between devices, from_everyone(): lax.all_to_all(jnp.broadcast_to(array[None], (size, *array.shape)), axis,...  13.1 us
    all_to_all x2, waiting for transfers between devices, from_everyone(): lax.all_to_all(jnp.broadcast_to(array[None], (size, *array.shape)), axis,...  9.99 us
    unnamed x19, local copies, waits for them, and re-layouts  9.27 us
    dot_general x2, matrix products, body(): jnp.dot(normed, piece, preferred_element_type=jnp.float32)  8.31 us
    dot_general x1, matrix products, body(): jnp.einsum('kgts,skd->tkgd', probs, values_proj, preferred_element_type=j...  7.65 us
  transfers between devices with their start and end apart: 5, of which 4 were waited for; matrix products, arithmetic and copies ran while one was open for 10% of the time, Pallas kernels for 0%

commit v1 on v0

v1 whole, which is shorter than its diff:
```python
import functools
import math

import jax
import jax.numpy as jnp
from jax import lax
from jax.experimental import pallas as pl
from jax.experimental.pallas import tpu as pltpu
from jax.sharding import PartitionSpec as P

HEAD = 128
discount = 0.999
trace_decay = 0.997
clip_range = 0.2
epsilon = 1e-05
rope_base = 500000.0

MESH = pl.DeviceIdType.MESH
F32 = jnp.float32
BF16 = jnp.bfloat16


def kernel(
    nz, nx,
    hid_hbm, wq_hbm, wk_hbm, wv_hbm, wo_hbm, cs_ref, sn_ref, vw_ref, rew_ref, old_ref, len_ref, term_ref,
    val_ref, adv_ref, loss_ref,
    hid, hown, wq, wkv, wo, att, accq, acckv, qs, ks, vs, bias, acco, rows_s, gae, red, lz, ly,
    lsem, rq, rkv, ro, ratt, rred, rlz, rly, rgae, ssem,
):
    D = hid.shape[1]
    T = hid.shape[0]
    R = wq_hbm.shape[0]
    FQ = wq_hbm.shape[1]
    FK = wk_hbm.shape[1]
    heads = FQ // HEAD
    nwin = gae.shape[0]
    ndp = 4 * nz
    half = nz // 2

    d = lax.axis_index("dp")
    m = lax.axis_index("mp")
    c = lax.rem(d, 2)
    z = lax.rem(d // 2, nz)
    yl = d // (2 * nz)
    yo = 1 - yl
    co = 1 - c
    xh = lax.rem(m, nx)
    yh = m // nx

    def dpi(yy, zz, cc):
        return (yy * nz + zz) * 2 + cc

    def zat(k):
        return lax.rem(z + (2 * nz + k), nz)

    def mpi(hh, k):
        return hh * nx + lax.rem(xh + (2 * nx + k), nx)

    def dev(dd, mm):
        return {"dp": dd, "mp": mm}

    sib = dev(dpi(yl, z, co), m)
    ypart = dev(dpi(yo, z, c), m)

    def zdev(k):
        return dev(dpi(yl, zat(k), c), m)

    def wslot(buf, idx, count=1):
        return buf.at[pl.ds(pl.multiple_of(idx * R, R), count * R)]

    class Stream:
        def __init__(self, buf, sems, send):
            self.buf, self.sems, self.sendsem = buf, sems, send

        def send(self, idx, to):
            ref = wslot(self.buf, idx)
            pltpu.make_async_remote_copy(ref, ref, ssem.at[self.sendsem], self.sems.at[idx], device_id=to, device_id_type=MESH).start()

        def wait(self, idx):
            ref = wslot(self.buf, idx)
            pltpu.make_async_remote_copy(ref, ref, ssem.at[self.sendsem], self.sems.at[idx], device_id=sib, device_id_type=MESH).wait_recv()

        def drain(self, count):
            ref = wslot(self.buf, 0, count)
            pltpu.make_async_remote_copy(ref, ref, ssem.at[self.sendsem], self.sems.at[0], device_id=sib, device_id_type=MESH).wait_send()

    SQ = Stream(wq, rq, 0)
    SKV = Stream(wkv, rkv, 1)
    SO = Stream(wo, ro, 2)

    own = pl.ds(pl.multiple_of(d * R, R), R)
    copies = [
        pltpu.make_async_copy(wk_hbm, wkv.at[own, pl.ds(0, FK)], lsem.at[0]),
        pltpu.make_async_copy(wv_hbm, wkv.at[own, pl.ds(FK, FK)], lsem.at[1]),
        pltpu.make_async_copy(wq_hbm, wq.at[own], lsem.at[2]),
        pltpu.make_async_copy(wo_hbm, wo.at[own], lsem.at[3]),
        pltpu.make_async_copy(hid_hbm, hid, lsem.at[4]),
        pltpu.make_async_copy(
            hid_hbm.at[:, pl.ds(pl.multiple_of(m * FQ, FQ), FQ)], hown, lsem.at[5]
        ),
    ]
    for copy in copies:
        copy.start()

    peers = [zdev(1), zdev(-1), sib, ypart]
    mpeers = [lax.rem(m + k, 2 * nx) for k in range(1, 2 * nx)]
    peers += [dev(d, mm) for mm in mpeers]
    for k in range(1, nwin):
        peers += [dev(lax.rem(d + k, ndp), m), dev(lax.rem(d + ndp - k, ndp), m)]
    barrier = pltpu.get_barrier_semaphore()
    for peer in peers:
        pl.semaphore_signal(barrier, inc=1, device_id=peer, device_id_type=MESH)

    gae[0, pl.ds(0, 1), :] = rew_ref[...]
    gae[0, pl.ds(1, 1), :] = old_ref[...]
    for copy in copies[:3]:
        copy.wait()
    pl.semaphore_wait(barrier, len(peers))

    SKV.send(d, ypart)
    for k in (1, -1):
        SQ.send(d, zdev(k))
        SKV.send(d, zdev(k))
    SQ.send(d, ypart)
    SKV.send(d, sib)
    SQ.send(d, sib)
    for k in range(1, nwin):
        pltpu.make_async_remote_copy(
            gae.at[0], gae.at[k], ssem.at[4], rgae.at[k],
            device_id=dev(lax.rem(d + ndp - k, ndp), m), device_id_type=MESH,
        ).start()
    other = dpi(yo, z, c)
    SKV.wait(other)
    for k in (1, -1):
        SKV.send(other, zdev(k))
    SKV.send(other, sib)

    def qkv_step(s, q_in=(True, True), kv_in=(True, True), q_out=(True, True), kv_out=(True, True)):
        for n, sgn in enumerate((1, -1)):
            zo = zat(-sgn * s)
            if q_in[n]:
                iq = dpi(yl, zo, c)
                SQ.wait(iq)
                if q_out[n]:
                    SQ.send(iq, zdev(sgn))
                SQ.send(iq, ypart)
                SQ.send(iq, sib)
            if kv_in[n]:
                for yy in (yl, yo):
                    ik = dpi(yy, zo, c)
                    SKV.wait(ik)
                    if kv_out[n]:
                        SKV.send(ik, zdev(sgn))
                    SKV.send(ik, sib)

    def across(zz):
        iq = dpi(yo, zz, c)
        SQ.wait(iq)
        SQ.send(iq, sib)

    def across_step(s):
        across(zat(-s))
        across(zat(s))

    def wo_first():
        SO.wait(other)
        for k in (1, -1):
            SO.send(d, zdev(k))
            SO.send(other, zdev(k))
        SO.send(d, sib)
        SO.send(other, sib)

    def wo_step(s):
        last = s == half
        for n, sgn in enumerate((1, -1)):
            zo = zat(-sgn * s)
            for r, yy in enumerate((yl, yo)):
                if last and r != n:
                    continue
                io = dpi(yy, zo, c)
                SO.wait(io)
                if not last and (s != half - 1 or r == n):
                    SO.send(io, zdev(sgn))
                SO.send(io, sib)

    def norm_rows(i, _):
        rr = pl.ds(pl.multiple_of(i * 32, 32), 32)
        x = hid[rr, :].astype(F32)
        ms = jnp.sum(x * x, axis=1, keepdims=True) * (1.0 / D)
        hid[rr, :] = (x * lax.rsqrt(ms + epsilon)).astype(BF16)
        return 0

    def mm_pos(zz):
        for yy in (yl, yo):
            i = dpi(yy, zz, co)
            SQ.wait(i)
            SKV.wait(i)
        lhs, rq_, rkv_ = [], [], []
        for yy in (0, 1):
            r0 = pl.ds(pl.multiple_of(dpi(yy, zz, 0) * R, 2 * R), 2 * R)
            lhs.append(hid[:, r0])
            rq_.append(wq[r0, :])
            rkv_.append(wkv[r0, :])
        lhs = jnp.concatenate(lhs, axis=1)
        accq[...] += jnp.dot(lhs, jnp.concatenate(rq_, axis=0), preferred_element_type=F32)
        acckv[...] += jnp.dot(lhs, jnp.concatenate(rkv_, axis=0), preferred_element_type=F32)

    def mm_range(lo, hi):
        def step(i, _):
            dist = (i + 1) // 2
            k = dist * (1 - 2 * lax.rem(i, 2))
            mm_pos(lax.rem(z + nz + k, nz))
            return 0
        lax.fori_loop(lo, hi, step, 0)

    kappa = math.log(discount * trace_decay)

    def marks():
        nl = len_ref.shape[1]
        si = lax.broadcasted_iota(jnp.int32, (nl, nl), 0)
        li = lax.broadcasted_iota(jnp.int32, (nl, nl), 1)
        lens = len_ref[...].astype(F32)
        ends_col = jnp.sum(jnp.where(li <= si, lens, 0.0), axis=1, keepdims=True)
        ends_row = jnp.sum(jnp.where(li == si, ends_col, 0.0), axis=0, keepdims=True)
        term_col = jnp.sum(jnp.where(li == si, term_ref[...].astype(F32), 0.0), axis=1, keepdims=True)
        for k in range(1, nwin):
            pltpu.make_async_remote_copy(
                gae.at[0], gae.at[k], ssem.at[4], rgae.at[k], device_id=sib, device_id_type=MESH
            ).wait_recv()
        lane = lax.broadcasted_iota(jnp.int32, (1, T), 1)
        base = (d * T).astype(F32)
        for k in range(nwin):
            pos = base + (lane + k * T).astype(F32)
            ep = jnp.sum(jnp.where(ends_col <= pos, 1.0, 0.0), axis=0, keepdims=True)
            hit = (ends_col - 1.0) == pos
            fin = jnp.sum(jnp.where(hit, 1.0, 0.0), axis=0, keepdims=True)
            stp = jnp.sum(jnp.where(hit, term_col, 0.0), axis=0, keepdims=True)
            rew = gae[k, pl.ds(0, 1), :]
            old = gae[k, pl.ds(1, 1), :]
            nxt = pltpu.roll(old, T - 1, 1)
            if k + 1 < nwin:
                nxt = jnp.where(lane == T - 1, gae[k + 1, pl.ds(1, 1), :][:, :1], nxt)
            booted = jnp.where(fin > 0.0, (1.0 - stp) * old, nxt)
            delta = rew + discount * booted - old
            rows_s[pl.ds(k, 1), :] = ep
            rows_s[pl.ds(8 + k, 1), :] = delta * jnp.exp((lane + k * T).astype(F32) * kappa)

        def rowblock(r, advr):
            n = 64
            sub = r * n + lax.broadcasted_iota(jnp.int32, (n, 1), 0)
            posc = base + sub.astype(F32)
            epc = jnp.sum(jnp.where(ends_row <= posc, 1.0, 0.0), axis=1, keepdims=True)
            ll = lax.broadcasted_iota(jnp.int32, (n, T), 1)
            ss = r * n + lax.broadcasted_iota(jnp.int32, (n, T), 0)
            same = rows_s[pl.ds(0, 1), :] == epc
            bias[pl.ds(pl.multiple_of(r * n, n), n), :] = jnp.where((ll <= ss) & same, 0.0, -1e30)
            tot = jnp.where((ll >= ss) & same, rows_s[pl.ds(8, 1), :], 0.0)
            for k in range(1, nwin):
                tot += jnp.where(rows_s[pl.ds(k, 1), :] == epc, rows_s[pl.ds(8 + k, 1), :], 0.0)
            col = jnp.sum(tot, axis=1, keepdims=True) * jnp.exp(sub.astype(F32) * (-kappa))
            return advr + jnp.sum(jnp.where(ll == ss, col, 0.0), axis=0, keepdims=True)

        adv_ref[...] = lax.fori_loop(0, T // 64, rowblock, jnp.zeros((1, T), F32))

    accq[...] = jnp.zeros_like(accq)
    acckv[...] = jnp.zeros_like(acckv)
    copies[4].wait()
    lax.fori_loop(0, T // 64, norm_rows, 0)
    qkv_step(1)
    across(z)
    lax.fori_loop(T // 64, T // 32, norm_rows, 0)
    qkv_step(2)
    across_step(1)
    marks()

    def mid(s, _):
        qkv_step(s)
        across_step(s - 1)
        mm_range(2 * s - 6, 2 * s - 4)
        return 0

    lax.fori_loop(3, half - 1, mid, 0)
    copies[3].wait()
    SO.send(d, ypart)
    qkv_step(half - 1, q_out=(True, False), kv_out=(False, True))
    across_step(half - 2)
    wo_first()
    qkv_step(half, q_in=(True, False), kv_in=(False, True), q_out=(False, False), kv_out=(False, False))
    across_step(half - 1)
    across(zat(half))
    mm_range(2 * half - 8, nz)

    def rope(x):
        return (x * cs_ref[...] + pltpu.roll(x, HEAD // 2, 1) * sn_ref[...]).astype(BF16)

    for h in range(heads):
        qs[h] = rope(accq[:, h * HEAD:(h + 1) * HEAD])
    ks[...] = rope(acckv[:, :FK])
    vs[...] = acckv[:, FK:].astype(BF16)

    scale = 1.0 / HEAD**0.5
    xp, xm = dev(d, mpi(yh, 1)), dev(d, mpi(yh, -1))
    yx = dev(d, mpi(1 - yh, 0))

    def att_send(o, h, to):
        i = o * heads + h
        pltpu.make_async_remote_copy(
            att.at[i], att.at[i], ssem.at[3], ratt.at[i], device_id=to, device_id_type=MESH
        ).start()

    def att_wait(o, h):
        i = o * heads + h
        pltpu.make_async_remote_copy(
            att.at[i], att.at[i], ssem.at[3], ratt.at[i], device_id=sib, device_id_type=MESH
        ).wait_recv()

    QB = 128

    def head(h):
        for i in range(T // QB):
            n = (i + 1) * QB
            sc = lax.dot_general(
                qs[h, i * QB:n, :], ks[:n, :], (((1,), (1,)), ((), ())), preferred_element_type=F32
            ) * scale + bias[i * QB:n, :n]
            big = jnp.max(sc, axis=1, keepdims=True)
            ex = jnp.exp(sc - big)
            pr = (ex / jnp.sum(ex, axis=1, keepdims=True)).astype(BF16)
            out = jnp.dot(pr, vs[:n, :], preferred_element_type=F32)
            att[m * heads + h, i * QB:n, :] = out.astype(BF16)

    def head_send(h):
        att_send(m, h, xp)
        att_send(m, h, xm)
        att_send(m, h, yx)

    def head_step(h, _):
        head(h)
        head_send(h)
        return 0

    lax.fori_loop(0, 2, head_step, 0)
    wo_step(1)
    lax.fori_loop(2, heads, head_step, 0)
    wo_step(2)

    def relay_near(h):
        for k in (-1, 1):
            o = mpi(yh, k)
            att_wait(o, h)
            if (h % 2 == 0) == (k == -1):
                att_send(o, h, xp if k == -1 else xm)

    def relay_y(h):
        o = mpi(1 - yh, 0)
        att_wait(o, h)
        att_send(o, h, xp)
        att_send(o, h, xm)

    def relay_far(h):
        for k in (-1, 1):
            o = mpi(1 - yh, k)
            att_wait(o, h)
            if (h % 2 == 0) == (k == -1):
                att_send(o, h, xp if k == -1 else xm)

    relay_near(0)
    relay_y(0)
    wo_step(3)
    relay_near(1)
    relay_y(1)
    wo_step(4)
    relay_near(2)
    relay_y(2)
    wo_step(5)
    relay_near(3)
    relay_y(3)
    wo_step(6)
    relay_far(0)
    wo_step(7)
    relay_far(1)
    wo_step(8)

    def wo_rest(i, _):
        for yy in (0, 1):
            SO.wait(dpi(yy, i, co))
        return 0

    lax.fori_loop(0, nz, wo_rest, 0)

    def project(o):
        lhs = jnp.concatenate([att[o * heads + h] for h in range(heads)], axis=1)
        r0 = pl.ds(pl.multiple_of(o * FQ, FQ), FQ)
        acco[...] += jnp.dot(lhs, wo[r0, :], preferred_element_type=F32)

    copies[5].wait()
    acco[...] = hown[...].astype(F32)
    project(m)
    relay_far(2)
    project(mpi(yh, 1))
    project(mpi(yh, -1))
    project(mpi(1 - yh, 0))
    relay_far(3)
    project(mpi(1 - yh, 1))
    project(mpi(1 - yh, -1))
    for h in range(heads):
        att_wait(mpi(yh, 2), h)
    project(mpi(yh, 2))
    for h in range(heads):
        att_wait(mpi(1 - yh, 2), h)
    project(mpi(1 - yh, 2))

    def sums(r, carry):
        n = 64
        x = acco[pl.ds(pl.multiple_of(r * n, n), n), :]
        ll = lax.broadcasted_iota(jnp.int32, (n, T), 1)
        ss = r * n + lax.broadcasted_iota(jnp.int32, (n, T), 0)
        sq = jnp.sum(x * x, axis=1, keepdims=True)
        hs = jnp.sum(x * vw_ref[...], axis=1, keepdims=True)
        a, b = carry
        a = a + jnp.sum(jnp.where(ll == ss, sq, 0.0), axis=0, keepdims=True)
        b = b + jnp.sum(jnp.where(ll == ss, hs, 0.0), axis=0, keepdims=True)
        return a, b

    zero = jnp.zeros((1, T), F32)
    sq, hs = lax.fori_loop(0, T // 64, sums, (zero, zero))
    red[m, pl.ds(0, 1), :] = sq
    red[m, pl.ds(1, 1), :] = hs
    for mm in mpeers:
        pltpu.make_async_remote_copy(
            red.at[m], red.at[m], ssem.at[5], rred.at[m], device_id=dev(d, mm), device_id_type=MESH
        ).start()
    for mm in mpeers:
        pltpu.make_async_remote_copy(
            red.at[mm], red.at[mm], ssem.at[5], rred.at[mm], device_id=sib, device_id_type=MESH
        ).wait_recv()
    tot = red[0]
    for k in range(1, 2 * nx):
        tot = tot + red[k]
    value = tot[1:2] * lax.rsqrt(tot[0:1] * (1.0 / D) + epsilon)
    val_ref[...] = value
    old = old_ref[...]
    returns = adv_ref[...] + old
    clipped = old + jnp.clip(value - old, -clip_range, clip_range)
    terms = jnp.maximum((value - returns) ** 2, (clipped - returns) ** 2)
    part = jnp.sum(terms, axis=1, keepdims=True)

    lz[z] = jnp.broadcast_to(part, lz.shape[1:])
    for k in range(1, nz):
        pltpu.make_async_remote_copy(
            lz.at[z], lz.at[z], ssem.at[6], rlz.at[z], device_id=zdev(k), device_id_type=MESH
        ).start()
    for k in range(1, nz):
        zz = zat(k)
        pltpu.make_async_remote_copy(
            lz.at[zz], lz.at[zz], ssem.at[6], rlz.at[zz], device_id=sib, device_id_type=MESH
        ).wait_recv()
    part = lz[0]
    for k in range(1, nz):
        part = part + lz[k]
    me = yl * 2 + c
    ly[me] = part
    quad = [(yl, co), (yo, c), (yo, co)]
    for yy, cc in quad:
        pltpu.make_async_remote_copy(
            ly.at[me], ly.at[me], ssem.at[7], rly.at[me], device_id=dev(dpi(yy, z, cc), m), device_id_type=MESH
        ).start()
    for yy, cc in quad:
        i = yy * 2 + cc
        pltpu.make_async_remote_copy(
            ly.at[i], ly.at[i], ssem.at[7], rly.at[i], device_id=sib, device_id_type=MESH
        ).wait_recv()
    total = (ly[0] + ly[1]) + (ly[2] + ly[3])
    loss_ref[...] = total[0:1] * (0.5 / (T * ndp))

    SQ.drain(ndp - 1)
    SKV.drain(ndp - 1)
    SO.drain(ndp - 1)

    def drain(buf, sem, count):
        ref = buf.at[pl.ds(0, count)]
        pltpu.make_async_remote_copy(
            ref, ref, ssem.at[sem], rred.at[0], device_id=sib, device_id_type=MESH
        ).wait_send()

    drain(att, 3, 28)
    drain(gae, 4, nwin - 1)
    drain(red, 5, 2 * nx - 1)
    drain(lz, 6, nz - 1)
    drain(ly, 7, 3)


def solution(mesh):
    ndp, nmp = mesh.shape["dp"], mesh.shape["mp"]
    nz, nx = ndp // 4, nmp // 2
    nwin = 5

    def body(hidden_in, w_query, w_key, w_value, w_out, value_weight, rewards, old_values, lengths, terminal):
        T, D = hidden_in.shape
        R, FQ = w_query.shape
        FK = w_key.shape[1]
        heads = FQ // HEAD
        nl = lengths.shape[0]
        half = HEAD // 2
        positions = (lax.axis_index("dp") * T + jnp.arange(T, dtype=jnp.int32)).astype(F32)
        freq = rope_base ** (-jnp.arange(half, dtype=F32) * 2.0 / HEAD)
        angles = positions[:, None] * jnp.concatenate([freq, freq])[None, :]
        sign = jnp.concatenate([-jnp.ones((half,), F32), jnp.ones((half,), F32)])
        cosine, sine = jnp.cos(angles), jnp.sin(angles) * sign[None, :]
        any_ = pl.BlockSpec(memory_space=pl.ANY)
        vmem = pl.BlockSpec(memory_space=pltpu.VMEM)
        dma = pltpu.SemaphoreType.DMA
        value, advantage, loss = pl.pallas_call(
            functools.partial(kernel, nz, nx),
            out_shape=(
                jax.ShapeDtypeStruct((1, T), F32),
                jax.ShapeDtypeStruct((1, T), F32),
                jax.ShapeDtypeStruct((1, 128), F32),
            ),
            in_specs=[any_] * 5 + [vmem] * 7,
            out_specs=(vmem, vmem, vmem),
            scratch_shapes=[
                pltpu.VMEM((T, D), BF16),
                pltpu.VMEM((T, FQ), BF16),
                pltpu.VMEM((D, FQ), BF16),
                pltpu.VMEM((D, 2 * FK), BF16),
                pltpu.VMEM((D, FQ), BF16),
                pltpu.VMEM((nmp * heads, T, HEAD), BF16),
                pltpu.VMEM((T, FQ), F32),
                pltpu.VMEM((T, 2 * FK), F32),
                pltpu.VMEM((heads, T, HEAD), BF16),
                pltpu.VMEM((T, HEAD), BF16),
                pltpu.VMEM((T, HEAD), BF16),
                pltpu.VMEM((T, T), F32),
                pltpu.VMEM((T, FQ), F32),
                pltpu.VMEM((16, T), F32),
                pltpu.VMEM((nwin, 8, T), F32),
                pltpu.VMEM((nmp, 8, T), F32),
                pltpu.VMEM((nz, 8, 128), F32),
                pltpu.VMEM((4, 8, 128), F32),
                dma((6,)),
                dma((ndp,)),
                dma((ndp,)),
                dma((ndp,)),
                dma((nmp * heads,)),
                dma((nmp,)),
                dma((nz,)),
                dma((4,)),
                dma((nwin,)),
                dma((8,)),
            ],
            compiler_params=pltpu.CompilerParams(collective_id=0, has_side_effects=True),
        )(
            hidden_in, w_query, w_key, w_value, w_out, cosine, sine,
            value_weight.reshape(1, FQ), rewards.reshape(1, T), old_values.reshape(1, T),
            lengths.reshape(1, nl), terminal.reshape(1, nl),
        )
        return value.reshape(T), advantage.reshape(T), loss[0, 0]

    return jax.shard_map(
        body,
        mesh=mesh,
        in_specs=(
            P("dp", None), P("dp", "mp"), P("dp", "mp"), P("dp", "mp"), P("dp", "mp"),
            P("mp"), P("dp"), P("dp"), P(), P(),
        ),
        out_specs=(P("dp"), P("dp"), P()),
        check_vma=False,
    )
```

time: 309 us -> 122 us (0.39)
  waiting for transfers between devices: 181 us -> 0 us
  Pallas kernels: 0 us -> 114 us
  blocking collectives: 28.7 us -> 0 us
  matrix products: 24.4 us -> 0 us
  other arithmetic: 21.7 us -> 2.55 us
  local copies, waits for them, and re-layouts: 19.1 us -> 2.49 us
  between operations: 18.7 us -> 2.34 us
  starting transfers between devices: 15.3 us -> 0 us
    all_gather x2 -> x0, waiting for transfers between devices: 171 us -> none  [the longest x1 125 us: sent_together(): whole = lax.all_gather(both, axis, axis=dim, tiled=True)]
    pallas_call x0 -> x1, Pallas kernels: none -> 114 us  [body(): pl.pallas_call(functools.partial(kernel, nz, nx), out_shape=(jax.ShapeDty...]
    all_to_all x1 -> x0, blocking collectives: 28.7 us -> none  [from_everyone(): lax.all_to_all(jnp.broadcast_to(array[None], (size, *array.shape)), axis,...]
    dot_general x6 -> x0, matrix products: 24.4 us -> none  [the longest x2 8.31 us: body(): jnp.dot(normed, piece, preferred_element_type=jnp.float32)]
    all_to_all x2 -> x0, starting transfers between devices: 13.1 us -> none  [from_everyone(): lax.all_to_all(jnp.broadcast_to(array[None], (size, *array.shape)), axis,...]
    all_to_all x2 -> x0, waiting for transfers between devices: 9.99 us -> none  [from_everyone(): lax.all_to_all(jnp.broadcast_to(array[None], (size, *array.shape)), axis,...]
    slice x35 -> x0, local copies, waits for them, and re-layouts: 7.74 us -> none  [the longest x26 3.61 us: joined_by_halves(): part[side::2]]
    reduce_sum x6 -> x0, other arithmetic: 7.14 us -> none  [the longest x1 3.14 us: body(): jnp.mean(states * states, 1, keepdims=True) + epsilon]
  transfers between devices with their start and end apart: 5 -> 0, of which waited for: 4 -> 0; matrix products, arithmetic and copies ran while one was open for 10% -> 0% of each run, Pallas kernels for 0% -> 0%
where the time goes in v1:
time: 122 us
  Pallas kernels  114 us (93%)
  other arithmetic  2.55 us (2%)
  local copies, waits for them, and re-layouts  2.49 us (2%)
  between operations  2.34 us (2%)
    pallas_call x1, Pallas kernels, body(): pl.pallas_call(functools.partial(kernel, nz, nx), out_shape=(jax.ShapeDty...  114 us
    unnamed x2, local copies, waits for them, and re-layouts  2.49 us
    mul x1, other arithmetic, body(): cosine, sine = (jnp.cos(angles), jnp.sin(angles) * sign[None, :])  2.46 us

profile of v1, /device:TPU:1, one launch (start us, length us, event | category | flops | bytes accessed | tf_op | source)
XLA Modules:
  0.0 121.5 jit_solution(1308035656898946537)
XLA Ops:
  0.6 0.1 pad_maximum_fusion
  0.7 2.5 %fusion = (f32[512,128]{1,0:T(8,128)}, f32[512,128]{1,0:T(8,128)}) fusion(f32[128]{0:T(128)} %constant.17.clone.1, f32[128]{0:T(128)S(1)} %pad_maximum_fusion, f32[512]{0:T(512)S(1)} %add_convert_fusion), kind=kLoop, calls=%fused_computation.2 | loop fusion | flops 131072 | bytes 527360 | tf_op jit(solution)/shard_map/mul | solution.py:508
  3.2 114.1 %shard_map.121 = (f32[1,512]{1,0:T(1,128)}, f32[1,512]{1,0:T(1,128)}, f32[1,128]{1,0:T(1,128)}) custom-call(bf16[512,4096]{1,0:T(8,128)(2,1)} %hid_hbm.1, bf16[64,512]{1,0:T(8,128)(2,1)} %wq_hbm.1, bf16[64,128]{1,0:T(8,128)(2,1)} %wk_hbm.1, bf16[64,128]{1,0:T(8,128)(2,1)} %wv_hbm.1, bf16[64,512]{1,0:T(8,128)(2,1)} %wo_hbm.1, ...), custom_call_target="tpu_custom_call" | custom-call | tf_op jit(solution)/shard_map/pallas_call | solution.py:512
  117.3 1.2 %copy.16 = f32[512]{0:T(512)} copy(f32[512]{0:T(512)} %bitcast.13) | data formatting | bytes 4096
  118.6 1.2 %copy.17 = f32[512]{0:T(512)} copy(f32[512]{0:T(512)} %bitcast.12) | data formatting | bytes 4096
  (2 shorter events, 0.0 us)

commit v2 on v1

v2 whole, which is shorter than its diff:
```python
import functools
import math

import jax
import jax.numpy as jnp
from jax import lax
from jax.experimental import pallas as pl
from jax.experimental.pallas import tpu as pltpu
from jax.sharding import PartitionSpec as P

HEAD = 128
discount = 0.999
trace_decay = 0.997
clip_range = 0.2
epsilon = 1e-05
rope_base = 500000.0

MESH = pl.DeviceIdType.MESH
F32 = jnp.float32
BF16 = jnp.bfloat16


CUT = 3


def att_numbers(heads):
    bulk, own = [0] * 5, {}
    kinds = ["near", "two", "y", "far", "last"]
    table = {}
    for kind, k, p in [(kind, k, p) for kind in kinds for k in ((-1, 1) if kind in ("near", "far") else (0,)) for p in range(2 * heads)]:
        turn = (p % 2 == 0) == (k == -1)
        passed = {
            "near": turn or p < CUT, "two": p < CUT, "y": p >= CUT, "far": turn and p >= CUT, "last": False
        }[kind]
        if passed:
            table[kind, k, p] = 5 + len(own)
            own[kind, k, p] = True
        else:
            table[kind, k, p] = kinds.index(kind)
            bulk[kinds.index(kind)] += 1
    return (lambda kind, k, p: table[kind, k, p]), bulk


def att_sems(heads):
    number, bulk = att_numbers(heads)
    return 1 + max(number(kind, k, p) for kind, k in (("near", -1), ("near", 1), ("two", 0), ("y", 0), ("far", -1), ("far", 1), ("last", 0)) for p in range(2 * heads))


def kernel(
    nz, nx,
    hid_hbm, wq_hbm, wk_hbm, wv_hbm, wo_hbm, cs_hbm, sn_hbm, vw_hbm, rew_hbm, old_hbm, len_hbm, term_hbm,
    out_hbm, loss_hbm,
    cs_ref, sn_ref, vw_ref, rew_ref, old_ref, len_ref, term_ref, val_ref, adv_ref, loss_ref,
    hid, hown, wq, wkv, wo, att, accq, acckv, qs, ks, vs, bias, acco, rows_s, gae, red, lz,
    lsem, rq, rkv, ro, ratt, rmisc, ssem,
):
    D = hid.shape[1]
    T = hid.shape[0]
    R = wq_hbm.shape[0]
    FQ = wq_hbm.shape[1]
    FK = wk_hbm.shape[1]
    heads = FQ // HEAD
    nwin = gae.shape[0]
    ndp = 4 * nz
    half = nz // 2

    d = lax.axis_index("dp")
    m = lax.axis_index("mp")
    c = lax.rem(d, 2)
    z = lax.rem(d // 2, nz)
    yl = d // (2 * nz)
    yo = 1 - yl
    co = 1 - c
    xh = lax.rem(m, nx)
    yh = m // nx

    def dpi(yy, zz, cc):
        return (yy * nz + zz) * 2 + cc

    def zat(k):
        return lax.rem(z + (2 * nz + k), nz)

    def mpi(hh, k):
        return hh * nx + lax.rem(xh + (2 * nx + k), nx)

    def dev(dd, mm):
        return {"dp": dd, "mp": mm}

    sib = dev(dpi(yl, z, co), m)
    ypart = dev(dpi(yo, z, c), m)

    def zdev(k):
        return dev(dpi(yl, zat(k), c), m)

    def wslot(buf, idx, n, count=1):
        return buf.at[pl.ds(pl.multiple_of(idx * n, n), count * n)]

    class Stream:
        def __init__(self, buf, send, n):
            self.buf, self.sendsem, self.n = buf, send, n

        def copy(self, ref, sem, to):
            return pltpu.make_async_remote_copy(ref, ref, ssem.at[self.sendsem], sem, device_id=to, device_id_type=MESH)

        def send(self, idx, sem, to):
            self.copy(wslot(self.buf, idx, self.n), sem, to).start()

        def wait(self, sem, count=1):
            self.copy(wslot(self.buf, 0, self.n, count), sem, sib).wait_recv()

        def drain(self, count):
            self.copy(wslot(self.buf, 0, self.n, count), ssem.at[self.sendsem], sib).wait_send()

    SQ = Stream(wq, 0, R // 2)
    SKV = Stream(wkv, 1, R)
    SO = Stream(wo, 2, R)

    own = pl.ds(pl.multiple_of(d * R, R), R)
    copies = [
        pltpu.make_async_copy(wk_hbm, wkv.at[own, pl.ds(0, FK)], lsem.at[0]),
        pltpu.make_async_copy(wv_hbm, wkv.at[own, pl.ds(FK, FK)], lsem.at[1]),
        pltpu.make_async_copy(wq_hbm, wq.at[own], lsem.at[2]),
        pltpu.make_async_copy(wo_hbm, wo.at[own], lsem.at[3]),
        pltpu.make_async_copy(hid_hbm, hid, lsem.at[4]),
        pltpu.make_async_copy(
            hid_hbm.at[:, pl.ds(pl.multiple_of(m * FQ, FQ), FQ)], hown, lsem.at[5]
        ),
    ]
    small = [
        pltpu.make_async_copy(src, dst, lsem.at[6 + i])
        for i, (src, dst) in enumerate([
            (rew_hbm, rew_ref), (old_hbm, old_ref), (len_hbm, len_ref), (term_hbm, term_ref),
            (vw_hbm, vw_ref), (cs_hbm, cs_ref), (sn_hbm, sn_ref),
        ])
    ]
    outs = [
        pltpu.make_async_copy(src, dst, lsem.at[13 + i])
        for i, (src, dst) in enumerate([(adv_ref, out_hbm.at[1]), (val_ref, out_hbm.at[0]), (loss_ref, loss_hbm)])
    ]
    for copy in copies[:3]:
        copy.start()

    kappa = math.log(discount * trace_decay)

    nl = len_ref.shape[1]

    def ends():
        si = lax.broadcasted_iota(jnp.int32, (nl, nl), 0)
        li = lax.broadcasted_iota(jnp.int32, (nl, nl), 1)
        lens = len_ref[...].astype(F32)
        ends_col = jnp.sum(jnp.where(li <= si, lens, 0.0), axis=1, keepdims=True)
        return si, li, ends_col

    base = (d * T).astype(F32)
    lane = lax.broadcasted_iota(jnp.int32, (1, T), 1)

    def landed(buf, send, sem, count):
        ref = buf.at[pl.ds(0, count)]
        pltpu.make_async_remote_copy(ref, ref, ssem.at[send], sem, device_id=sib, device_id_type=MESH).wait_recv()

    def first_marks():
        si, li, ends_col = ends()
        rows_s[pl.ds(6, 1), pl.ds(0, nl)] = jnp.sum(jnp.where(li == si, ends_col, 0.0), axis=0, keepdims=True)
        pos = base + lane.astype(F32)
        rows_s[pl.ds(0, 1), :] = jnp.sum(jnp.where(ends_col <= pos, 1.0, 0.0), axis=0, keepdims=True)

    xp, xm = dev(d, mpi(yh, 1)), dev(d, mpi(yh, -1))
    yx = dev(d, mpi(1 - yh, 0))
    peers = [zdev(1), zdev(-1), sib, ypart, xp, xm, yx]
    mpeers = [lax.rem(m + k, 2 * nx) for k in range(1, 2 * nx)]
    barrier = pltpu.get_barrier_semaphore()
    for peer in peers:
        pl.semaphore_signal(barrier, inc=1, device_id=peer, device_id_type=MESH)
    for copy in copies[4:] + small + copies[3:4]:
        copy.start()
    for copy in copies[:3]:
        copy.wait()
    pl.semaphore_wait(barrier, len(peers))

    sgn = 2 * c - 1
    onward = zdev(sgn)

    other, theirs, both = dpi(yo, z, c), dpi(yl, z, co), dpi(yo, z, co)

    def q_ring(s, n, i):
        return rq.at[(s - 1) * 4 + n * 2 + i]

    def q_cross(k, n, i):
        return rq.at[4 * half - 2 + k * 4 + n * 2 + i]

    def q_sib(k):
        return rq.at[8 * half + k]

    def kv_ring(s, n, r):
        return rkv.at[(s - 1) * 4 + n * 2 + r]

    def kv_sib(k):
        return rkv.at[4 * half - 2 + k]

    def o_ring(s, n, r):
        return ro.at[(s - 1) * 4 + n * 2 + r]

    KV_Y, KV_THEIRS, KV_BOTH = (rkv.at[5 * half - 1 + k] for k in range(3))
    O_Y, O_THEIRS, O_BOTH, O_SIB = (ro.at[4 * half - 2 + k] for k in range(4))
    Q_THEIRS = rq.at[9 * half + 1]

    def core_of(n):
        return c if n == 0 else co

    def zat_(k):
        return lax.rem(z + 2 * nz + k, nz)

    def nothing():
        pass

    def kv_pass(s, zo, n, r, on):
        ik = dpi(yl if r == 0 else yo, zo, core_of(n))
        SKV.wait(kv_ring(s, n, r))
        if on:
            SKV.send(ik, kv_ring(s + 1, n, r), onward)
        SKV.send(ik, kv_sib(s - 1), sib)

    def across(k, n, i):
        iq = dpi(yo, zat_(-sgn * k), core_of(n)) * 2 + i
        SQ.wait(q_cross(k, n, i))
        SQ.send(iq, q_sib(k), sib)

    def qkv_step(s, pieces, cores=(0, 1), out=(0, 1)):
        zo = zat_(-sgn * s)
        todo = list(pieces)
        first = isinstance(s, int) and s == 1
        crossing = [(n, i) for n in ((0,) if first else (0, 1)) for i in (0, 1)]

        def work():
            if todo:
                todo.pop(0)()

        def cross_next():
            if crossing:
                across(s - 1, *crossing.pop(0))

        for n in cores:
            for i in (0, 1):
                iq = dpi(yl, zo, core_of(n)) * 2 + i
                SQ.wait(q_ring(s, n, i))
                if n in out:
                    SQ.send(iq, q_ring(s + 1, n, i), onward)
                SQ.send(iq, q_cross(s, n, i), ypart)
                SQ.send(iq, q_sib(s), sib)
                work()
            kv_pass(s, zo, n, 0, n in out)
            cross_next()
            work()
        for n in cores:
            kv_pass(s, zo, n, 1, n in out)
            cross_next()
            work()
        while crossing:
            cross_next()
        while todo:
            work()

    def wo_first():
        SO.send(d, o_ring(1, 0, 0), onward)
        SO.wait(O_THEIRS)
        SO.send(theirs, o_ring(1, 1, 0), onward)
        SO.wait(O_Y)
        SO.send(other, o_ring(1, 0, 1), onward)
        SO.send(other, O_BOTH, sib)
        SO.wait(O_BOTH)
        SO.send(both, o_ring(1, 1, 1), onward)

    def wo_step(s):
        zo = zat_(-sgn * s)
        for n in (0,) if s == half else (0, 1):
            for r, yy in enumerate((yl, yo)):
                io = dpi(yy, zo, core_of(n))
                SO.wait(o_ring(s, n, r))
                if s < half - 1 or (s == half - 1 and n == 0):
                    SO.send(io, o_ring(s + 1, n, r), onward)
                SO.send(io, O_SIB, sib)

    def norm_rows(i, _):
        rr = pl.ds(pl.multiple_of(i * 32, 32), 32)
        x = hid[rr, :].astype(F32)
        ms = jnp.sum(x * x, axis=1, keepdims=True) * (1.0 / D)
        hid[rr, :] = (x * lax.rsqrt(ms + epsilon)).astype(BF16)
        return 0

    def rows_of(zz):
        return [pl.ds(pl.multiple_of(dpi(yy, zz, 0) * R, 2 * R), 2 * R) for yy in (0, 1)]

    def mm_q(zz):
        lhs = jnp.concatenate([hid[:, r] for r in rows_of(zz)], axis=1)
        rhs = jnp.concatenate([wq[r, :] for r in rows_of(zz)], axis=0)
        accq[...] += jnp.dot(lhs, rhs, preferred_element_type=F32)

    def mm_kv(zz):
        lhs = jnp.concatenate([hid[:, r] for r in rows_of(zz)], axis=1)
        rhs = jnp.concatenate([wkv[r, :] for r in rows_of(zz)], axis=0)
        acckv[...] += jnp.dot(lhs, rhs, preferred_element_type=F32)

    def opp_q(k):
        SQ.wait(q_sib(k), 8)
        mm_q(zat_(sgn * k))

    def opp_kv(k):
        SKV.wait(kv_sib(k - 1), 4)
        mm_kv(zat_(sgn * k))

    NB = 64

    def block_of(r):
        sub = r * NB + lax.broadcasted_iota(jnp.int32, (NB, 1), 0)
        posc = base + sub.astype(F32)
        epc = jnp.sum(jnp.where(rows_s[pl.ds(6, 1), pl.ds(0, nl)] <= posc, 1.0, 0.0), axis=1, keepdims=True)
        ll = lax.broadcasted_iota(jnp.int32, (NB, T), 1)
        ss = r * NB + lax.broadcasted_iota(jnp.int32, (NB, T), 0)
        return sub, epc, ll, ss

    def bias_rows(r, _):
        sub, epc, ll, ss = block_of(r)
        same = rows_s[pl.ds(0, 1), :] == epc
        bias[pl.ds(pl.multiple_of(r * NB, NB), NB), :] = jnp.where((ll <= ss) & same, 0.0, -1e30)
        return 0

    def gae_send():
        for k in range(1, nwin):
            pltpu.make_async_remote_copy(
                gae.at[0], gae.at[k], ssem.at[4], rmisc.at[0],
                device_id=dev(lax.rem(d + ndp - k, ndp), m), device_id_type=MESH,
            ).start()

    def advantages():
        landed(gae, 4, rmisc.at[0], nwin - 1)
        si, li, ends_col = ends()
        term_col = jnp.sum(jnp.where(li == si, term_ref[...].astype(F32), 0.0), axis=1, keepdims=True)
        for k in range(nwin):
            pos = base + (lane + k * T).astype(F32)
            ep = jnp.sum(jnp.where(ends_col <= pos, 1.0, 0.0), axis=0, keepdims=True)
            hit = (ends_col - 1.0) == pos
            fin = jnp.sum(jnp.where(hit, 1.0, 0.0), axis=0, keepdims=True)
            stp = jnp.sum(jnp.where(hit, term_col, 0.0), axis=0, keepdims=True)
            rew = gae[k, pl.ds(0, 1), :]
            old = gae[k, pl.ds(1, 1), :]
            nxt = pltpu.roll(old, T - 1, 1)
            if k + 1 < nwin:
                nxt = jnp.where(lane == T - 1, gae[k + 1, pl.ds(1, 1), :][:, :1], nxt)
            booted = jnp.where(fin > 0.0, (1.0 - stp) * old, nxt)
            delta = rew + discount * booted - old
            rows_s[pl.ds(k, 1), :] = ep
            rows_s[pl.ds(8 + k, 1), :] = delta * jnp.exp((lane + k * T).astype(F32) * kappa)

        def rowblock(r, advr):
            sub, epc, ll, ss = block_of(r)
            same = rows_s[pl.ds(0, 1), :] == epc
            tot = jnp.where((ll >= ss) & same, rows_s[pl.ds(8, 1), :], 0.0)
            for k in range(1, nwin):
                tot += jnp.where(rows_s[pl.ds(k, 1), :] == epc, rows_s[pl.ds(8 + k, 1), :], 0.0)
            col = jnp.sum(tot, axis=1, keepdims=True) * jnp.exp(sub.astype(F32) * (-kappa))
            return advr + jnp.sum(jnp.where(ll == ss, col, 0.0), axis=0, keepdims=True)

        adv_ref[...] = lax.fori_loop(0, T // NB, rowblock, jnp.zeros((1, T), F32))
        outs[0].start()

    SKV.send(d, KV_Y, ypart)
    for i in (0, 1):
        SQ.send(2 * d + i, Q_THEIRS, sib)
    SKV.send(d, KV_THEIRS, sib)
    for i in (0, 1):
        SQ.send(2 * d + i, q_ring(1, 0, i), onward)
    SKV.send(d, kv_ring(1, 0, 0), onward)
    for i in (0, 1):
        SQ.send(2 * d + i, q_cross(0, 0, i), ypart)
    accq[...] = jnp.zeros_like(accq)
    acckv[...] = jnp.zeros_like(acckv)
    for copy in small + copies[4:5]:
        copy.wait()
    gae[0, pl.ds(0, 1), :] = rew_ref[...]
    gae[0, pl.ds(1, 1), :] = old_ref[...]
    first_marks()
    SQ.wait(Q_THEIRS, 2)
    for i in (0, 1):
        SQ.send(2 * theirs + i, q_ring(1, 1, i), onward)
    SKV.wait(KV_THEIRS)
    SKV.send(theirs, kv_ring(1, 1, 0), onward)
    lax.fori_loop(0, 4, norm_rows, 0)
    def norms(lo, hi):
        return functools.partial(lax.fori_loop, lo, hi, norm_rows, 0)

    def other_kv():
        SKV.wait(KV_Y)
        SKV.send(other, kv_ring(1, 0, 1), onward)
        SKV.send(other, KV_BOTH, sib)

    def both_kv():
        SKV.wait(KV_BOTH)
        SKV.send(both, kv_ring(1, 1, 1), onward)

    qkv_step(1, [norms(4, 5), other_kv, both_kv, norms(5, 6), norms(6, 7), norms(7, 8), norms(8, 9), norms(9, 10)])
    def biases(lo, hi):
        return functools.partial(lax.fori_loop, lo, hi, bias_rows, 0)

    def own_q():
        SQ.wait(q_sib(0), 2)
        mm_q(z)

    def own_kv():
        mm_kv(z)

    qkv_step(2, [norms(10, 11), norms(11, 12), norms(12, 13), norms(13, 14), norms(14, 15), norms(15, 16), own_kv, own_q])
    def pieces_at(s):
        k = s - 2
        zm = zat_(-sgn * k)
        return [nothing, lambda: mm_q(zm), nothing, lambda: mm_kv(zm), nothing, lambda: opp_q(k), nothing, lambda: opp_kv(k)]

    share = T // NB // (half - 4)

    def mid(s, _):
        extra = pieces_at(s)
        extra[0] = functools.partial(lax.fori_loop, (s - 3) * share, (s - 2) * share, bias_rows, 0)
        qkv_step(s, extra)
        return 0

    lax.fori_loop(3, half - 1, mid, 0)
    copies[3].wait()
    SO.send(d, O_THEIRS, sib)
    SO.send(d, O_Y, ypart)
    qkv_step(half - 1, pieces_at(half - 1), out=(0,))
    wo_first()
    qkv_step(half, pieces_at(half), cores=(0,), out=())
    mm_kv(zat_(-sgn * (half - 1)))
    mm_q(zat_(-sgn * (half - 1)))
    for i in (0, 1):
        across(half, 0, i)
    opp_kv(half - 1)
    opp_q(half - 1)
    SKV.wait(kv_sib(half - 1), 2)
    mm_kv(zat_(half))
    wo_step(1)
    SQ.wait(q_sib(half), 4)
    mm_q(zat_(half))

    low = lax.broadcasted_iota(jnp.int32, (T // 2, HEAD), 1) < HEAD // 2

    def spread(ref, sign):
        table = ref[...]
        turned = pltpu.roll(table, HEAD // 2, 1)
        first, second = jnp.where(low, table, turned), jnp.where(low, turned, table)
        if sign:
            first, second = jnp.where(low, -first, first), jnp.where(low, -second, second)
        return first, second

    cosines, sines = spread(cs_ref, False), spread(sn_ref, True)

    def rope(load, store):
        for n in (0, 1):
            x = load(slice(n * T // 2, (n + 1) * T // 2))
            store(slice(n * T // 2, (n + 1) * T // 2), (x * cosines[n] + pltpu.roll(x, HEAD // 2, 1) * sines[n]).astype(BF16))

    def put_q(h):
        def store(r, x):
            qs[h, r, :] = x
        return store

    def put_k(r, x):
        ks[r, :] = x

    for h in range(heads):
        rope(lambda r: accq[r, h * HEAD:(h + 1) * HEAD], put_q(h))
    rope(lambda r: acckv[r, :FK], put_k)
    vs[...] = acckv[:, FK:].astype(BF16)

    scale = 1.0 / HEAD**0.5

    number, bulk = att_numbers(heads)

    def att_copy(o, p, kind, k, to):
        i = o * (2 * heads) + p
        n = number(kind, k, p)
        return pltpu.make_async_remote_copy(
            att.at[i], att.at[i], ssem.at[3], ratt.at[n], device_id=to, device_id_type=MESH
        )

    def att_send(o, p, kind, k, to):
        att_copy(o, p, kind, k, to).start()

    def att_wait(o, p, kind, k):
        if number(kind, k, p) >= len(bulk):
            att_copy(o, p, kind, k, sib).wait_recv()

    def att_rest(n):
        landed(att, 3, ratt.at[n], bulk[n])

    QB = 128

    def piece_send(p):
        att_send(m, p, "near", -1, xp)
        att_send(m, p, "near", 1, xm)
        att_send(m, p, "y", 0, yx)

    def head_step(h):
        for i in range(T // QB):
            n = (i + 1) * QB
            sc = lax.dot_general(
                qs[h, i * QB:n, :], ks[:n, :], (((1,), (1,)), ((), ())), preferred_element_type=F32
            ) * scale + bias[i * QB:n, :n]
            big = jnp.max(sc, axis=1, keepdims=True)
            ex = jnp.exp(sc - big)
            pr = (ex / jnp.sum(ex, axis=1, keepdims=True)).astype(BF16)
            out = jnp.dot(pr, vs[:n, :], preferred_element_type=F32)
            r = 2 * i // (T // QB)
            low_row = i * QB - r * (T // 2)
            att[m * (2 * heads) + 2 * h + r, low_row:low_row + QB, :] = out.astype(BF16)
            if (i + 1) * 2 % (T // QB) == 0:
                piece_send(2 * h + r)

    head_step(0)
    head_step(1)
    gae_send()
    wo_step(2)
    for h in range(2, heads):
        head_step(h)

    cut = CUT

    def relay_near(p):
        for k in (-1, 1):
            o = mpi(yh, k)
            att_wait(o, p, "near", k)
            if (p % 2 == 0) == (k == -1):
                att_send(o, p, "two", 0, xp if k == -1 else xm)
            if p < cut:
                att_send(o, p, "far", k, yx)

    def relay_two(p):
        o = mpi(yh, 2)
        att_wait(o, p, "two", 0)
        if p < cut:
            att_send(o, p, "last", 0, yx)

    def relay_y(p):
        o = mpi(1 - yh, 0)
        att_wait(o, p, "y", 0)
        if p >= cut:
            att_send(o, p, "far", -1, xp)
            att_send(o, p, "far", 1, xm)

    def relay_far(p):
        for k in (-1, 1):
            o = mpi(1 - yh, k)
            att_wait(o, p, "far", k)
            if p >= cut and (p % 2 == 0) == (k == -1):
                att_send(o, p, "last", 0, xp if k == -1 else xm)

    for p in range(cut):
        relay_near(p)
    wo_step(3)
    advantages()
    wo_step(4)
    for p in range(cut, 2 * heads):
        relay_near(p)
        relay_y(p)
    wo_step(5)
    for p in range(cut):
        relay_two(p)
    wo_step(6)
    relay_far(3)
    relay_far(4)
    wo_step(7)
    relay_far(5)
    relay_far(6)
    wo_step(8)
    relay_far(7)

    SO.wait(O_SIB, 4 * half - 2)
    def project(o):
        r0 = pl.ds(pl.multiple_of(o * FQ, FQ), FQ)
        for r in (0, 1):
            lhs = jnp.concatenate([att[o * (2 * heads) + 2 * h + r] for h in range(heads)], axis=1)
            acco[r * T // 2:(r + 1) * T // 2, :] += jnp.dot(lhs, wo[r0, :], preferred_element_type=F32)

    copies[5].wait()
    acco[...] = hown[...].astype(F32)
    project(m)
    att_rest(0)
    project(mpi(yh, 1))
    project(mpi(yh, -1))
    att_rest(1)
    project(mpi(yh, 2))
    att_rest(2)
    project(mpi(1 - yh, 0))
    att_rest(3)
    project(mpi(1 - yh, 1))
    project(mpi(1 - yh, -1))
    att_rest(4)
    project(mpi(1 - yh, 2))

    def sums(r, carry):
        n = 64
        x = acco[pl.ds(pl.multiple_of(r * n, n), n), :]
        ll = lax.broadcasted_iota(jnp.int32, (n, T), 1)
        ss = r * n + lax.broadcasted_iota(jnp.int32, (n, T), 0)
        sq = jnp.sum(x * x, axis=1, keepdims=True)
        hs = jnp.sum(x * vw_ref[...], axis=1, keepdims=True)
        a, b = carry
        a = a + jnp.sum(jnp.where(ll == ss, sq, 0.0), axis=0, keepdims=True)
        b = b + jnp.sum(jnp.where(ll == ss, hs, 0.0), axis=0, keepdims=True)
        return a, b

    zero = jnp.zeros((1, T), F32)
    sq, hs = lax.fori_loop(0, T // 64, sums, (zero, zero))
    red[m, pl.ds(0, 1), :] = sq
    red[m, pl.ds(1, 1), :] = hs
    for mm in mpeers:
        pltpu.make_async_remote_copy(
            red.at[m], red.at[m], ssem.at[5], rmisc.at[1], device_id=dev(d, mm), device_id_type=MESH
        ).start()
    landed(red, 5, rmisc.at[1], 2 * nx - 1)
    tot = red[0]
    for k in range(1, 2 * nx):
        tot = tot + red[k]
    value = tot[1:2] * lax.rsqrt(tot[0:1] * (1.0 / D) + epsilon)
    val_ref[...] = value
    outs[1].start()
    old = old_ref[...]
    returns = adv_ref[...] + old
    clipped = old + jnp.clip(value - old, -clip_range, clip_range)
    terms = jnp.maximum((value - returns) ** 2, (clipped - returns) ** 2)
    part = jnp.sum(terms, axis=1, keepdims=True)

    lz[d] = jnp.broadcast_to(part, lz.shape[1:])
    far = sorted(range(nz), key=lambda k: -min(k, nz - k))
    for k in far:
        for yy in (yo, yl):
            for cc in (co, c):
                if k == 0 and yy is yl and cc is c:
                    continue
                pltpu.make_async_remote_copy(
                    lz.at[d], lz.at[d], ssem.at[6], rmisc.at[2],
                    device_id=dev(dpi(yy, zat(k), cc), m), device_id_type=MESH,
                ).start()

    landed(lz, 6, rmisc.at[2], ndp - 1)
    total = lz[0]
    for k in range(1, ndp):
        total = total + lz[k]
    loss_ref[...] = total * (0.5 / (T * ndp))
    outs[2].start()

    SQ.drain(2 * (ndp - 1))
    SKV.drain(ndp - 1)
    SO.drain(ndp - 1)

    def drain(buf, sem, count):
        ref = buf.at[pl.ds(0, count)]
        pltpu.make_async_remote_copy(
            ref, ref, ssem.at[sem], rmisc.at[1], device_id=sib, device_id_type=MESH
        ).wait_send()

    drain(att, 3, 14 * heads)
    drain(gae, 4, nwin - 1)
    drain(red, 5, 2 * nx - 1)
    drain(lz, 6, ndp - 1)
    for copy in outs:
        copy.wait()


def solution(mesh):
    ndp, nmp = mesh.shape["dp"], mesh.shape["mp"]
    nz, nx = ndp // 4, nmp // 2
    nwin = 5

    def body(hidden_in, w_query, w_key, w_value, w_out, value_weight, rewards, old_values, lengths, terminal):
        T, D = hidden_in.shape
        R, FQ = w_query.shape
        FK = w_key.shape[1]
        heads = FQ // HEAD
        nl = lengths.shape[0]
        half = HEAD // 2
        freq = rope_base ** (-jnp.arange(half, dtype=F32) * 2.0 / HEAD)
        upper = (jnp.arange(HEAD, dtype=jnp.int32) // half) * (T // 2)
        positions = lax.axis_index("dp") * T + jnp.arange(T // 2, dtype=jnp.int32)
        angles = (positions[:, None] + upper[None, :]).astype(F32) * jnp.concatenate([freq, freq])[None, :]
        cosine, sine = jnp.cos(angles), jnp.sin(angles)
        any_ = pl.BlockSpec(memory_space=pl.ANY)
        dma = pltpu.SemaphoreType.DMA
        out, loss = pl.pallas_call(
            functools.partial(kernel, nz, nx),
            out_shape=(
                jax.ShapeDtypeStruct((2, 1, T), F32),
                jax.ShapeDtypeStruct((1, 128), F32),
            ),
            in_specs=[any_] * 12,
            out_specs=(any_, any_),
            scratch_shapes=[
                pltpu.VMEM((T // 2, HEAD), F32),
                pltpu.VMEM((T // 2, HEAD), F32),
                pltpu.VMEM((1, FQ), F32),
                pltpu.VMEM((1, T), F32),
                pltpu.VMEM((1, T), F32),
                pltpu.VMEM((1, nl), jnp.int32),
                pltpu.VMEM((1, nl), jnp.int32),
                pltpu.VMEM((1, T), F32),
                pltpu.VMEM((1, T), F32),
                pltpu.VMEM((1, 128), F32),
                pltpu.VMEM((T, D), BF16),
                pltpu.VMEM((T, FQ), BF16),
                pltpu.VMEM((D, FQ), BF16),
                pltpu.VMEM((D, 2 * FK), BF16),
                pltpu.VMEM((D, FQ), BF16),
                pltpu.VMEM((nmp * 2 * heads, T // 2, HEAD), BF16),
                pltpu.VMEM((T, FQ), F32),
                pltpu.VMEM((T, 2 * FK), F32),
                pltpu.VMEM((heads, T, HEAD), BF16),
                pltpu.VMEM((T, HEAD), BF16),
                pltpu.VMEM((T, HEAD), BF16),
                pltpu.VMEM((T, T), F32),
                pltpu.VMEM((T, FQ), F32),
                pltpu.VMEM((16, T), F32),
                pltpu.VMEM((nwin, 2, T), F32),
                pltpu.VMEM((nmp, 2, T), F32),
                pltpu.VMEM((ndp, 1, 128), F32),
                dma((16,)),
                dma((9 * nz // 2 + 2,)),
                dma((5 * nz // 2 + 2,)),
                dma((2 * nz + 2,)),
                dma((att_sems(heads),)),
                dma((3,)),
                dma((7,)),
            ],
            compiler_params=pltpu.CompilerParams(collective_id=0, has_side_effects=True),
        )(
            hidden_in, w_query, w_key, w_value, w_out, cosine, sine,
            value_weight.reshape(1, FQ), rewards.reshape(1, T), old_values.reshape(1, T),
            lengths.reshape(1, nl), terminal.reshape(1, nl),
        )
        return out[0, 0], out[1, 0], loss[0, 0]

    return jax.shard_map(
        body,
        mesh=mesh,
        in_specs=(
            P("dp", None), P("dp", "mp"), P("dp", "mp"), P("dp", "mp"), P("dp", "mp"),
            P("mp"), P("dp"), P("dp"), P(), P(),
        ),
        out_specs=(P("dp"), P("dp"), P()),
        check_vma=False,
    )
```

time: 122 us -> 98 us (0.80)
  Pallas kernels: 114 us -> 92.6 us
  local copies, waits for them, and re-layouts: 2.49 us -> 1.27 us
    pallas_call x1, Pallas kernels: 114 us -> 92.6 us  [body(): pl.pallas_call(functools.partial(kernel, nz, nx), out_shape=(jax.ShapeDty...]
    unnamed x2 -> x0, local copies, waits for them, and re-layouts: 2.49 us -> none
    mul x1, other arithmetic: 2.46 us -> 0.01 us  [body(): upper = jnp.arange(HEAD, dtype=jnp.int32) // half * (T // 2)]
    slice x0 -> x1, local copies, waits for them, and re-layouts: none -> 1.27 us  [body(): return (out[0, 0], out[1, 0], loss[0, 0])]
    sin x0 -> x1, other arithmetic: none -> 1.24 us  [body(): cosine, sine = (jnp.cos(angles), jnp.sin(angles))]
where the time goes in v2:
time: 98 us; the launch traced here: 97.7 us
  Pallas kernels  92.6 us (94%)
  between operations  2.48 us (3%)
  other arithmetic  1.34 us (1%)
  local copies, waits for them, and re-layouts  1.27 us (1%)
    pallas_call x1, Pallas kernels, body(): pl.pallas_call(functools.partial(kernel, nz, nx), out_shape=(jax.ShapeDty...  92.6 us

profile of v2, /device:TPU:1, one launch (start us, length us, event | category | flops | bytes accessed | tf_op | source)
XLA Modules:
  0.0 97.7 jit_solution(13310904486815352111)
XLA Ops:
  0.7 0.1 pad_maximum_fusion
  0.7 1.2 %fusion = (f32[256,128]{1,0:T(8,128)}, f32[256,128]{1,0:T(8,128)}) fusion(f32[128]{0:T(128)S(1)} %pad_maximum_fusion, s32[128]{0:T(128)S(1)} %fusion.2, s32[256]{0:T(256)S(1)} %iota_add_fusion), kind=kLoop, calls=%fused_computation.1 | loop fusion | flops 98304 | bytes 264192 | tf_op jit(solution)/shard_map/sin | solution.py:685
  2.0 92.6 %shard_map.121 = (f32[2,1,512]{2,1,0:T(1,128)}, f32[1,128]{1,0:T(1,128)}) custom-call(bf16[512,4096]{1,0:T(8,128)(2,1)} %hid_hbm.1, bf16[64,512]{1,0:T(8,128)(2,1)} %wq_hbm.1, bf16[64,128]{1,0:T(8,128)(2,1)} %wk_hbm.1, bf16[64,128]{1,0:T(8,128)(2,1)} %wv_hbm.1, bf16[64,512]{1,0:T(8,128)(2,1)} %wo_hbm.1, f32[256,128]{1,0:T(8,128)} %get-tuple-element.10.cs_hbm, ...), custom_call_target="tpu_custom_call" | custom-call | tf_op jit(solution)/shard_map/pallas_call | solution.py:688
  94.6 1.3 %fusion.3 = (f32[1,1,512]{2,1,0:T(1,128)}, f32[1,1,512]{2,1,0:T(1,128)}) fusion(f32[2,1,512]{2,1,0:T(1,128)} %get-tuple-element.5), kind=kLoop, calls=%fused_computation.11 | loop fusion | bytes 8192 | tf_op jit(solution)/shard_map/slice | solution.py:738
  (3 shorter events, 0.0 us)

commit v3 on v2

--- a/solution.py
+++ b/solution.py
@@ -28,7 +28,7 @@
     kinds = ["near", "two", "y", "far", "last"]
     table = {}
     for kind, k, p in [(kind, k, p) for kind in kinds for k in ((-1, 1) if kind in ("near", "far") else (0,)) for p in range(2 * heads)]:
-        turn = (p % 2 == 0) == (k == -1)
+        turn = k == -1
         passed = {
             "near": turn or p < CUT, "two": p < CUT, "y": p >= CUT, "far": turn and p >= CUT, "last": False
         }[kind]
@@ -48,9 +48,9 @@
 
 def kernel(
     nz, nx,
-    hid_hbm, wq_hbm, wk_hbm, wv_hbm, wo_hbm, cs_hbm, sn_hbm, vw_hbm, rew_hbm, old_hbm, len_hbm, term_hbm,
+    hid_hbm, wq_hbm, wk_hbm, wv_hbm, wo_hbm, fr_hbm, vw_hbm, rew_hbm, old_hbm, len_hbm, term_hbm,
     out_hbm, loss_hbm,
-    cs_ref, sn_ref, vw_ref, rew_ref, old_ref, len_ref, term_ref, val_ref, adv_ref, loss_ref,
+    cs_ref, sn_ref, fr_ref, vw_ref, rew_ref, old_ref, len_ref, term_ref, val_ref, adv_ref, loss_ref,
     hid, hown, wq, wkv, wo, att, accq, acckv, qs, ks, vs, bias, acco, rows_s, gae, red, lz,
     lsem, rq, rkv, ro, ratt, rmisc, ssem,
 ):
@@ -130,11 +130,11 @@
         pltpu.make_async_copy(src, dst, lsem.at[6 + i])
         for i, (src, dst) in enumerate([
             (rew_hbm, rew_ref), (old_hbm, old_ref), (len_hbm, len_ref), (term_hbm, term_ref),
-            (vw_hbm, vw_ref), (cs_hbm, cs_ref), (sn_hbm, sn_ref),
+            (vw_hbm, vw_ref), (fr_hbm, fr_ref),
         ])
     ]
     outs = [
-        pltpu.make_async_copy(src, dst, lsem.at[13 + i])
+        pltpu.make_async_copy(src, dst, lsem.at[12 + i])
         for i, (src, dst) in enumerate([(adv_ref, out_hbm.at[1]), (val_ref, out_hbm.at[0]), (loss_ref, loss_hbm)])
     ]
     for copy in copies[:3]:
@@ -165,6 +165,13 @@
         rows_s[pl.ds(0, 1), :] = jnp.sum(jnp.where(ends_col <= pos, 1.0, 0.0), axis=0, keepdims=True)
 
     xp, xm = dev(d, mpi(yh, 1)), dev(d, mpi(yh, -1))
+
+    def away(p, k=1):
+        return k * (1 - 2 * lax.rem(c + p, 2))
+
+    def xdev(k):
+        return dev(d, mpi(yh, k))
+
     yx = dev(d, mpi(1 - yh, 0))
     peers = [zdev(1), zdev(-1), sib, ypart, xp, xm, yx]
     mpeers = [lax.rem(m + k, 2 * nx) for k in range(1, 2 * nx)]
@@ -324,6 +331,16 @@
         bias[pl.ds(pl.multiple_of(r * NB, NB), NB), :] = jnp.where((ll <= ss) & same, 0.0, -1e30)
         return 0
 
+    def angle_rows(r, _):
+        n = 32
+        rr = lax.broadcasted_iota(jnp.int32, (n, HEAD), 0)
+        upper = jnp.where(lax.broadcasted_iota(jnp.int32, (n, HEAD), 1) < HEAD // 2, 0, T // 2)
+        angles = (rr + upper + (d * T + r * n)).astype(F32) * fr_ref[...]
+        at = pl.ds(pl.multiple_of(r * n, n), n)
+        cs_ref[at, :] = jnp.cos(angles)
+        sn_ref[at, :] = jnp.sin(angles)
+        return 0
+
     def gae_send():
         for k in range(1, nwin):
             pltpu.make_async_remote_copy(
@@ -372,6 +389,11 @@
     SKV.send(d, kv_ring(1, 0, 0), onward)
     for i in (0, 1):
         SQ.send(2 * d + i, q_cross(0, 0, i), ypart)
+    SQ.wait(Q_THEIRS, 2)
+    for i in (0, 1):
+        SQ.send(2 * theirs + i, q_ring(1, 1, i), onward)
+    SKV.wait(KV_THEIRS)
+    SKV.send(theirs, kv_ring(1, 1, 0), onward)
     accq[...] = jnp.zeros_like(accq)
     acckv[...] = jnp.zeros_like(acckv)
     for copy in small + copies[4:5]:
@@ -379,11 +401,6 @@
     gae[0, pl.ds(0, 1), :] = rew_ref[...]
     gae[0, pl.ds(1, 1), :] = old_ref[...]
     first_marks()
-    SQ.wait(Q_THEIRS, 2)
-    for i in (0, 1):
-        SQ.send(2 * theirs + i, q_ring(1, 1, i), onward)
-    SKV.wait(KV_THEIRS)
-    SKV.send(theirs, kv_ring(1, 1, 0), onward)
     lax.fori_loop(0, 4, norm_rows, 0)
     def norms(lo, hi):
         return functools.partial(lax.fori_loop, lo, hi, norm_rows, 0)
@@ -419,6 +436,8 @@
     def mid(s, _):
         extra = pieces_at(s)
         extra[0] = functools.partial(lax.fori_loop, (s - 3) * share, (s - 2) * share, bias_rows, 0)
+        extra[2] = lambda: angle_rows((s - 3) * 2, 0)
+        extra[4] = lambda: angle_rows((s - 3) * 2 + 1, 0)
         qkv_step(s, extra)
         return 0
 
@@ -466,8 +485,9 @@
     def put_k(r, x):
         ks[r, :] = x
 
-    for h in range(heads):
+    def rope_q(h):
         rope(lambda r: accq[r, h * HEAD:(h + 1) * HEAD], put_q(h))
+
     rope(lambda r: acckv[r, :FK], put_k)
     vs[...] = acckv[:, FK:].astype(BF16)
 
@@ -495,8 +515,8 @@
     QB = 128
 
     def piece_send(p):
-        att_send(m, p, "near", -1, xp)
-        att_send(m, p, "near", 1, xm)
+        att_send(m, p, "near", -1, xdev(away(p)))
+        att_send(m, p, "near", 1, xdev(away(p, -1)))
         att_send(m, p, "y", 0, yx)
 
     def head_step(h):
@@ -515,21 +535,26 @@
             if (i + 1) * 2 % (T // QB) == 0:
                 piece_send(2 * h + r)
 
+    rope_q(0)
     head_step(0)
+    rope_q(1)
     head_step(1)
     gae_send()
+    rope_q(2)
+    head_step(2)
     wo_step(2)
-    for h in range(2, heads):
+    for h in range(3, heads):
+        rope_q(h)
         head_step(h)
 
     cut = CUT
 
     def relay_near(p):
         for k in (-1, 1):
-            o = mpi(yh, k)
+            o = mpi(yh, away(p, k))
             att_wait(o, p, "near", k)
-            if (p % 2 == 0) == (k == -1):
-                att_send(o, p, "two", 0, xp if k == -1 else xm)
+            if k == -1:
+                att_send(o, p, "two", 0, xdev(away(p)))
             if p < cut:
                 att_send(o, p, "far", k, yx)
 
@@ -543,15 +568,15 @@
         o = mpi(1 - yh, 0)
         att_wait(o, p, "y", 0)
         if p >= cut:
-            att_send(o, p, "far", -1, xp)
-            att_send(o, p, "far", 1, xm)
+            att_send(o, p, "far", -1, xdev(away(p)))
+            att_send(o, p, "far", 1, xdev(away(p, -1)))
 
     def relay_far(p):
         for k in (-1, 1):
-            o = mpi(1 - yh, k)
+            o = mpi(1 - yh, away(p, k))
             att_wait(o, p, "far", k)
-            if p >= cut and (p % 2 == 0) == (k == -1):
-                att_send(o, p, "last", 0, xp if k == -1 else xm)
+            if p >= cut and k == -1:
+                att_send(o, p, "last", 0, xdev(away(p)))
 
     for p in range(cut):
         relay_near(p)
@@ -609,7 +634,7 @@
         return a, b
 
     zero = jnp.zeros((1, T), F32)
-    sq, hs = lax.fori_loop(0, T // 64, sums, (zero, zero))
+    sq, hs = lax.fori_loop(0, T // 64, sums, (zero, zero), unroll=True)
     red[m, pl.ds(0, 1), :] = sq
     red[m, pl.ds(1, 1), :] = hs
     for mm in mpeers:
@@ -678,11 +703,7 @@
         heads = FQ // HEAD
         nl = lengths.shape[0]
         half = HEAD // 2
-        freq = rope_base ** (-jnp.arange(half, dtype=F32) * 2.0 / HEAD)
-        upper = (jnp.arange(HEAD, dtype=jnp.int32) // half) * (T // 2)
-        positions = lax.axis_index("dp") * T + jnp.arange(T // 2, dtype=jnp.int32)
-        angles = (positions[:, None] + upper[None, :]).astype(F32) * jnp.concatenate([freq, freq])[None, :]
-        cosine, sine = jnp.cos(angles), jnp.sin(angles)
+        freq = rope_base ** (-(jnp.arange(HEAD, dtype=jnp.int32) % half).astype(F32) * 2.0 / HEAD)
         any_ = pl.BlockSpec(memory_space=pl.ANY)
         dma = pltpu.SemaphoreType.DMA
         out, loss = pl.pallas_call(
@@ -691,11 +712,12 @@
                 jax.ShapeDtypeStruct((2, 1, T), F32),
                 jax.ShapeDtypeStruct((1, 128), F32),
             ),
-            in_specs=[any_] * 12,
+            in_specs=[any_] * 11,
             out_specs=(any_, any_),
             scratch_shapes=[
                 pltpu.VMEM((T // 2, HEAD), F32),
                 pltpu.VMEM((T // 2, HEAD), F32),
+                pltpu.VMEM((1, HEAD), F32),
                 pltpu.VMEM((1, FQ), F32),
                 pltpu.VMEM((1, T), F32),
                 pltpu.VMEM((1, T), F32),
@@ -721,7 +743,7 @@
                 pltpu.VMEM((nwin, 2, T), F32),
                 pltpu.VMEM((nmp, 2, T), F32),
                 pltpu.VMEM((ndp, 1, 128), F32),
-                dma((16,)),
+                dma((15,)),
                 dma((9 * nz // 2 + 2,)),
                 dma((5 * nz // 2 + 2,)),
                 dma((2 * nz + 2,)),
@@ -731,7 +753,7 @@
             ],
             compiler_params=pltpu.CompilerParams(collective_id=0, has_side_effects=True),
         )(
-            hidden_in, w_query, w_key, w_value, w_out, cosine, sine,
+            hidden_in, w_query, w_key, w_value, w_out, freq.reshape(1, HEAD),
             value_weight.reshape(1, FQ), rewards.reshape(1, T), old_values.reshape(1, T),
             lengths.reshape(1, nl), terminal.reshape(1, nl),
         )

time: 98 us -> 96.7 us (0.987)
    sin x1 -> x0, other arithmetic: 1.24 us -> none  [body(): cosine, sine = (jnp.cos(angles), jnp.sin(angles))]
where the time goes in v3:
time: 96.7 us; the launch traced here: 96.4 us
  Pallas kernels  92.2 us (95%)
  between operations  2.4 us (2%)
  local copies, waits for them, and re-layouts  1.26 us (1%)
    pallas_call x1, Pallas kernels, body(): pl.pallas_call(functools.partial(kernel, nz, nx), out_shape=(jax.ShapeDty...  92.2 us

profile of v3, /device:TPU:1, one launch (start us, length us, event | category | flops | bytes accessed | tf_op | source)
XLA Modules:
  0.0 96.4 jit_solution(17987777469291646123)
XLA Ops:
  0.6 0.5 fusion.3.fr_hbm
  1.2 92.2 %shard_map.121 = (f32[2,1,512]{2,1,0:T(1,128)}, f32[1,128]{1,0:T(1,128)}) custom-call(bf16[512,4096]{1,0:T(8,128)(2,1)} %hid_hbm.1, bf16[64,512]{1,0:T(8,128)(2,1)} %wq_hbm.1, bf16[64,128]{1,0:T(8,128)(2,1)} %wk_hbm.1, bf16[64,128]{1,0:T(8,128)(2,1)} %wv_hbm.1, bf16[64,512]{1,0:T(8,128)(2,1)} %wo_hbm.1, f32[1,128]{1,0:T(1,128)} %fusion.3.fr_hbm, ...), custom_call_target="tpu_custom_call" | custom-call | tf_op jit(solution)/shard_map/pallas_call | solution.py:709
  93.4 1.3 %fusion.4 = (f32[1,1,512]{2,1,0:T(1,128)}, f32[1,1,512]{2,1,0:T(1,128)}) fusion(f32[2,1,512]{2,1,0:T(1,128)} %get-tuple-element.5), kind=kLoop, calls=%fused_computation.5 | loop fusion | bytes 8192 | tf_op jit(solution)/shard_map/slice | solution.py:760

commit v4 on v3

--- a/solution.py
+++ b/solution.py
@@ -3,6 +3,7 @@
 
 import jax
 import jax.numpy as jnp
+import numpy as np
 from jax import lax
 from jax.experimental import pallas as pl
 from jax.experimental.pallas import tpu as pltpu
@@ -335,7 +336,7 @@
         n = 32
         rr = lax.broadcasted_iota(jnp.int32, (n, HEAD), 0)
         upper = jnp.where(lax.broadcasted_iota(jnp.int32, (n, HEAD), 1) < HEAD // 2, 0, T // 2)
-        angles = (rr + upper + (d * T + r * n)).astype(F32) * fr_ref[...]
+        angles = (rr + upper + (d * T + r * n)).astype(F32) * jnp.concatenate([fr_ref[...], fr_ref[...]], axis=1)
         at = pl.ds(pl.multiple_of(r * n, n), n)
         cs_ref[at, :] = jnp.cos(angles)
         sn_ref[at, :] = jnp.sin(angles)
@@ -368,6 +369,7 @@
             rows_s[pl.ds(k, 1), :] = ep
             rows_s[pl.ds(8 + k, 1), :] = delta * jnp.exp((lane + k * T).astype(F32) * kappa)
 
+    def advantages_sum():
         def rowblock(r, advr):
             sub, epc, ll, ss = block_of(r)
             same = rows_s[pl.ds(0, 1), :] == epc
@@ -540,9 +542,9 @@
     rope_q(1)
     head_step(1)
     gae_send()
+    wo_step(2)
     rope_q(2)
     head_step(2)
-    wo_step(2)
     for h in range(3, heads):
         rope_q(h)
         head_step(h)
@@ -583,6 +585,7 @@
     wo_step(3)
     advantages()
     wo_step(4)
+    advantages_sum()
     for p in range(cut, 2 * heads):
         relay_near(p)
         relay_y(p)
@@ -595,8 +598,8 @@
     wo_step(7)
     relay_far(5)
     relay_far(6)
+    relay_far(7)
     wo_step(8)
-    relay_far(7)
 
     SO.wait(O_SIB, 4 * half - 2)
     def project(o):
@@ -703,7 +706,7 @@
         heads = FQ // HEAD
         nl = lengths.shape[0]
         half = HEAD // 2
-        freq = rope_base ** (-(jnp.arange(HEAD, dtype=jnp.int32) % half).astype(F32) * 2.0 / HEAD)
+        freq = np.power(rope_base, -np.arange(half, dtype=np.float64) * 2.0 / HEAD).astype(np.float32)
         any_ = pl.BlockSpec(memory_space=pl.ANY)
         dma = pltpu.SemaphoreType.DMA
         out, loss = pl.pallas_call(
@@ -717,7 +720,7 @@
             scratch_shapes=[
                 pltpu.VMEM((T // 2, HEAD), F32),
                 pltpu.VMEM((T // 2, HEAD), F32),
-                pltpu.VMEM((1, HEAD), F32),
+                pltpu.VMEM((1, HEAD // 2), F32),
                 pltpu.VMEM((1, FQ), F32),
                 pltpu.VMEM((1, T), F32),
                 pltpu.VMEM((1, T), F32),
@@ -753,7 +756,7 @@
             ],
             compiler_params=pltpu.CompilerParams(collective_id=0, has_side_effects=True),
         )(
-            hidden_in, w_query, w_key, w_value, w_out, freq.reshape(1, HEAD),
+            hidden_in, w_query, w_key, w_value, w_out, jnp.asarray(freq.reshape(1, half)),
             value_weight.reshape(1, FQ), rewards.reshape(1, T), old_values.reshape(1, T),
             lengths.reshape(1, nl), terminal.reshape(1, nl),
         )

time: 96.7 us -> 97.7 us (1.010)
  Pallas kernels: 92.2 us -> 93.8 us
    pallas_call x1, Pallas kernels: 92.2 us -> 93.8 us  [body(): pl.pallas_call(functools.partial(kernel, nz, nx), out_shape=(jax.ShapeDty...]
where the time goes in v4:
time: 97.7 us; the launch traced here: 97.4 us
  Pallas kernels  93.8 us (96%)
  between operations  2.4 us (2%)
  local copies, waits for them, and re-layouts  1.26 us (1%)
    pallas_call x1, Pallas kernels, body(): pl.pallas_call(functools.partial(kernel, nz, nx), out_shape=(jax.ShapeDty...  93.8 us

profile of v4, /device:TPU:1, one launch (start us, length us, event | category | flops | bytes accessed | tf_op | source)
XLA Modules:
  0.0 97.4 jit_solution(13124086334650864426)
XLA Ops:
  0.6 93.8 %shard_map.130 = (f32[2,1,512]{2,1,0:T(1,128)}, f32[1,128]{1,0:T(1,128)}) custom-call(bf16[512,4096]{1,0:T(8,128)(2,1)} %hid_hbm.1, bf16[64,512]{1,0:T(8,128)(2,1)} %wq_hbm.1, bf16[64,128]{1,0:T(8,128)(2,1)} %wk_hbm.1, bf16[64,128]{1,0:T(8,128)(2,1)} %wv_hbm.1, bf16[64,512]{1,0:T(8,128)(2,1)} %wo_hbm.1, f32[1,64]{1,0:T(1,128)} %constant.2.clone.fr_hbm, ...), custom_call_target="tpu_custom_call" | custom-call | tf_op jit(solution)/shard_map/pallas_call | solution.py:712
  94.4 1.3 %fusion = (f32[1,1,512]{2,1,0:T(1,128)}, f32[1,1,512]{2,1,0:T(1,128)}) fusion(f32[2,1,512]{2,1,0:T(1,128)} %get-tuple-element.5), kind=kLoop, calls=%fused_computation | loop fusion | bytes 8192 | tf_op jit(solution)/shard_map/slice | solution.py:763
